TPU v7x, 32 devices: a whole 2x2x4 slice. The times are simulated.
32 devices in a mesh: row: 2 (over core), col: 8 (over z, x), grp: 2 (over y).
Axes of the slice: x: 2, y: 2, z: 4, core: 2. Of those that a mesh axis runs over, the one named last changes fastest.
Arguments:
- momentum: float32 [2, 4096, 16384], P('grp', 'row', 'col'), may hold values from -6 to 6
- gradient: bfloat16 [2, 4096, 16384], P('grp', 'row', 'col'), may hold values from -6 to 6
- factor_q: float32 [2, 16384, 256], P('grp', 'col', 'row'), may hold values from -0.046875 to 0.046875
- weights: float32 [2, 4096, 16384], P(None, 'row', ('col', 'grp')), may hold values from -6 to 6
- tokens: bfloat16 [256, 4096], P(None, 'row'), may hold values from -0.08984375 to 0.08984375
Outputs:
- momentum_out: float32 [2, 4096, 16384], P('grp', 'row', 'col')
- factor_out: float32 [2, 16384, 256], P('grp', 'col', 'row')
- weights_out: float32 [2, 4096, 16384], P(None, 'row', ('col', 'grp'))
- hidden: bfloat16 [256, 16384], P('row', ('col', 'grp'))
All inputs are finite; a program needn't handle non-finite values.
Results may differ from a plain program's by a relative error of at most 0.0061.
Values may be sent and summed in bfloat16 or wider, within the bound.
No kernel may reach another device: no remote copies, remote signals or barrier semaphores. Data moves between devices by JAX's collectives and lax.ppermute only.
A program may use at most 128 MiB of HBM per device.

v0:
```python
import math

import jax
import jax.numpy as jnp
from jax import lax
from jax.sharding import PartitionSpec as P

D = 4096
HID = 16384


feedback = 0.05
epsilon = 1e-06


def gram_of(left_rows):
    return jnp.dot(left_rows.T, left_rows, precision=lax.Precision.HIGHEST)


def orthonormal(gram_sum, left_rows):
    factor_l = jnp.linalg.cholesky(gram_sum)
    return jax.scipy.linalg.solve_triangular(factor_l, left_rows.T, lower=True).T


def local(momentum, gradient, factor_q, weights, tokens):
    buffer = momentum[0] + gradient[0].astype(jnp.float32)
    buffer_h = buffer.astype(jnp.bfloat16)
    partial_value = jnp.dot(
        buffer_h,
        lax.all_gather(factor_q[0].astype(jnp.bfloat16), "row", axis=1, tiled=True),
        preferred_element_type=jnp.float32,
    )
    left_full = lax.psum(partial_value, "col")
    gram_sum = lax.psum(gram_of(left_full), "row")
    left_h = orthonormal(gram_sum, left_full).astype(jnp.bfloat16)
    right_part = lax.dot_general(
        buffer_h, left_h, (((0,), (0,)), ((), ())), preferred_element_type=jnp.float32
    )
    rank_share = factor_q.shape[2]
    right_full = lax.psum(right_part, "row")
    squares = lax.psum(jnp.sum(right_full * right_full, axis=0), "col")
    new_q = right_full / jnp.sqrt(squares + epsilon)
    q_share = lax.dynamic_slice_in_dim(new_q, lax.axis_index("row") * rank_share, rank_share, 1)
    right_h = right_full.astype(jnp.bfloat16)
    new_q_h = new_q.astype(jnp.bfloat16)
    feedback_term = lax.dot_general(
        left_h, right_h, (((1,), (1,)), ((), ())), preferred_element_type=jnp.float32
    )
    mom_new = buffer - feedback * feedback_term
    left_both = lax.all_gather(left_h[None], "grp", axis=0, tiled=True)
    right_both = lax.all_to_all(new_q_h[None], "grp", split_axis=1, concat_axis=0, tiled=True)
    step_size = 0.4 * math.sqrt(max(D, HID))
    low_rank = lax.dot_general(
        left_both, right_both, (((2,), (2,)), ((0,), (0,))), preferred_element_type=jnp.float32
    )
    new_weights = weights - step_size * low_rank
    weights_h = new_weights.astype(jnp.bfloat16)
    dec_parts = lax.psum_scatter(
        jnp.einsum("bd,pdh->bph", tokens, weights_h, preferred_element_type=jnp.float32),
        "row",
        scatter_dimension=0,
        tiled=True,
    )
    hidden = (jax.nn.silu(dec_parts[:, 0]) * dec_parts[:, 1]).astype(jnp.bfloat16)
    return (mom_new[None], q_share[None], new_weights, hidden)


def solution(mesh):
    in_specs = (
        P("grp", "row", "col"),
        P("grp", "row", "col"),
        P("grp", "col", "row"),
        P(None, "row", ("col", "grp")),
        P(None, "row"),
    )
    out_specs = (
        P("grp", "row", "col"),
        P("grp", "col", "row"),
        P(None, "row", ("col", "grp")),
        P("row", ("col", "grp")),
    )
    return jax.shard_map(local, mesh=mesh, in_specs=in_specs, out_specs=out_specs, check_vma=False)
```

profile of v0, /device:TPU:0, one launch (start us, length us, event | category | flops | bytes accessed | tf_op | source)
XLA Modules:
  0.0 394.1 jit_solution(15597743867390131542)
XLA Ops:
  7.2 2.1 convert_element_type.31
  9.4 12.2 %all-gather.5.cloned.1.call-done = bf16[1,2048,256]{2,1,0:T(8,128)(2,1)} async-done(((bf16[1,2048,128]{2,1,0:T(8,128)(2,1)}), bf16[1,2048,256]{2,1,0:T(8,128)(2,1)}) %all-gather.5.cloned.1.call-update) | async-done | bytes 1048592 | tf_op jit(solution)/shard_map/all_gather | solution.py:30
  21.6 12.3 %fusion.9 = f32[2048,256]{1,0:T(8,128)} fusion(bf16[1,2048,256]{2,1,0:T(8,128)(2,1)} %all-gather.5.cloned.1.call-done, f32[1,2048,2048]{2,1,0:T(8,128)} %param.5, bf16[1,2048,2048]{2,1,0:T(8,128)(2,1)} %param.6), kind=kOutput, calls=%fused_computation.18 | convolution fusion | flops 2160066560 | bytes 28311552 | tf_op jit(solution)/shard_map/dot_general | solution.py:28
  34.0 103.6 %all-reduce.5.cloned.1.call-done = f32[2048,256]{1,0:T(8,128)} async-done(((f32[2048,256]{1,0:T(8,128)}), f32[2048,256]{1,0:T(8,128)}) %all-reduce.5.cloned.1.call-update) | async-done | bytes 2097168 | tf_op jit(solution)/shard_map/psum | solution.py:33
  137.6 6.4 %fusion.25 = f32[256,256]{0,1:T(8,128)} fusion(f32[2048,256]{1,0:T(8,128)} %all-reduce.5.cloned.1.call-done), kind=kOutput, calls=%fused_computation.56 | convolution fusion | flops 1610612736 | bytes 2359296 | tf_op jit(solution)/shard_map/dot_general | solution.py:17
  144.0 0.6 all-reduce.9.cloned.1.call-start
  144.6 17.1 %all-reduce.7.cloned.1.call-done = f32[256,256]{0,1:T(8,128)} async-done(((f32[256,256]{0,1:T(8,128)}), f32[256,256]{0,1:T(8,128)}) %all-reduce.7.cloned.1.call-update) | async-done | bytes 262160 | tf_op jit(solution)/shard_map/psum | solution.py:34
  161.6 1.1 copy.21
  162.7 1.0 fusion.16
  163.7 0.7 copy-done.10
  164.4 11.7 %cholesky.50 = f32[128,128]{1,0:T(8,128)S(1)} custom-call(f32[128,128]{1,0:T(8,128)S(1)} %cholesky.118), custom_call_target="Cholesky" | custom-call | tf_op jit(solution)/shard_map/jit(cholesky)/cholesky | solution.py:21
  176.2 9.8 %custom-call.15 = f32[1,128,128]{1,2,0:T(8,128)S(1)} custom-call(f32[1,128,128]{2,1,0:T(8,128)S(1)} %get-tuple-element.39), custom_call_target="InvertDiagBlocksLowerTriangular" | custom-call | tf_op jit(solution)/shard_map/jit(cholesky)/cholesky | solution.py:21
  186.0 1.0 constant_dynamic-update-slice_fusion
  187.0 1.1 convolution_subtract_fusion.1
  188.2 11.7 %cholesky.105 = f32[128,128]{1,0:T(8,128)S(1)} custom-call(f32[128,128]{1,0:T(8,128)S(1)} %convolution_subtract_fusion.1), custom_call_target="Cholesky" | custom-call | tf_op jit(solution)/shard_map/jit(cholesky)/cholesky | solution.py:21
  199.9 0.7 compare_reduce_fusion
  202.0 1.0 select_select_fusion
  203.0 5.4 %while.1 = (s32[]{:T(128)}, f32[256,256]{1,0:T(8,128)S(1)}, s32[2,2]{1,0:T(2,128)S(1)}, f32[2,128,128]{2,1,0:T(8,128)}, s32[]{:T(128)}) while((s32[]{:T(128)}, f32[256,256]{1,0:T(8,128)S(1)}, s32[2,2]{1,0:T(2,128)S(1)}, f32[2,128,128]{2,1,0:T(8,128)}, s32[]{:T(128)}) %tuple.32), condition=%wide.while_cond, body=%wide.while_body.sunk | while | flops 2 | bytes 132205 | solution.py:22
  203.2 0.6 fusion.35
  203.8 2.0 bitcast_dynamic-update-slice_fusion.2
  205.8 0.6 fusion.35
  206.4 2.0 bitcast_dynamic-update-slice_fusion.2
  208.4 20.5 %custom-call.16 = f32[2,128,128]{1,2,0:T(8,128)S(1)} custom-call(f32[2,128,128]{2,1,0:T(8,128)} %get-tuple-element.11), custom_call_target="InvertDiagBlocksLowerTriangular" | custom-call | tf_op jit(solution)/shard_map/jit(_solve_triangular)/triangular_solve | solution.py:22
  228.9 1.1 fusion.24
  230.0 1.8 convolution_subtract_fusion
  231.8 1.1 convolution_convert_fusion
  232.9 13.1 %fusion.15 = f32[2048,256]{1,0:T(8,128)} fusion(bf16[128,2048]{1,0:T(8,128)(2,1)S(1)} %convolution_convert_fusion, bf16[128,2048]{1,0:T(8,128)(2,1)S(1)} %get-tuple-element.42, f32[1,2048,2048]{2,1,0:T(8,128)} %param.5, bf16[1,2048,2048]{2,1,0:T(8,128)(2,1)} %param.6), kind=kOutput, calls=%fused_computation.29 | convolution fusion | flops 2162163712 | bytes 28311552 | tf_op jit(solution)/shard_map/dot_general | solution.py:36
  246.1 1.0 copy-done.6
  247.1 1.0 fusion.14
  248.1 20.6 %all-reduce.9.cloned.1.call-done = f32[2048,256]{1,0:T(8,128)} async-done(((f32[2048,256]{1,0:T(8,128)}), f32[2048,256]{1,0:T(8,128)}) %all-reduce.9.cloned.1.call-update) | async-done | bytes 2097168 | tf_op jit(solution)/shard_map/psum | solution.py:40
  268.7 2.0 multiply_reduce_fusion
  270.8 21.8 %psum.31 = f32[256]{0:T(256)S(1)} all-reduce(f32[256]{0:T(256)S(1)} %multiply_reduce_fusion), channel_id=1, replica_groups=mesh['row'=2,'col'=8,'grp'=2] {'col'}, use_global_device_ids=true, to_apply=%region_8.9 | all-reduce | flops 256 | bytes 2048 | tf_op jit(solution)/shard_map/psum | solution.py:41
  292.6 1.5 convert_bitcast_fusion
  294.1 12.9 %copy.33 = bf16[1,2048,256]{2,0,1:T(2,128)(2,1)} copy(bf16[1,2048,256]{2,1,0:T(8,128)(2,1)S(1)} %get-tuple-element.32) | data formatting | bytes 2097152 | tf_op jit(solution)/shard_map/broadcast_in_dim | solution.py:51
  307.0 0.5 broadcast.117
  307.5 12.6 %reduce.12 = bf16[2048,256]{1,0:T(8,128)(2,1)} reduce(bf16[2048,1,256]{2,1,0:T(2,128)(2,1)} %bitcast.81, bf16[]{:T(256)} %broadcast.117), dimensions={1}, to_apply=%bitcast.70.reduce_sub_computation | reduce | bytes 2097154
  320.2 2.2 reshape.56
  322.3 4.4 %all-to-all-start = ((bf16[2,2,131072]{2,1,0:T(2,128)(2,1)}), bf16[2,2,131072]{2,1,0:T(2,128)(2,1)}, u32[]{:S(2)}, u32[]{:S(2)}) async-start(bf16[2,2,131072]{2,1,0:T(2,128)(2,1)} %reshape.56), calls=%async_computation | async-start | bytes 2097152 | tf_op jit(solution)/shard_map/all_to_all | solution.py:51
  326.8 4.3 %copy.30 = bf16[4096,256]{1,0:T(8,128)(2,1)} copy(bf16[4096,256]{0,1:T(8,128)(2,1)} %all-gather.7.cloned.1.call-done) | data formatting | bytes 4194304 | tf_op jit(solution)/shard_map/all_gather | solution.py:50
  331.2 6.2 %all-to-all-done = bf16[2,2,131072]{2,1,0:T(2,128)(2,1)} async-done(((bf16[2,2,131072]{2,1,0:T(2,128)(2,1)}), bf16[2,2,131072]{2,1,0:T(2,128)(2,1)}, u32[]{:S(2)}, u32[]{:S(2)}) %all-to-all-start) | async-done | bytes 1048608 | tf_op jit(solution)/shard_map/all_to_all | solution.py:51
  337.4 3.0 reshape.57
  340.4 1.9 copy.31
  342.6 14.3 %multiply_subtract_fusion = f32[2,2048,1024]{2,1,0:T(8,128)} fusion(f32[2,2048,1024]{2,1,0:T(8,128)} %param.8, bf16[2,2048,256]{2,1,0:T(8,128)(2,1)S(1)} %bitcast.79, bf16[2,1024,256]{2,1,0:T(8,128)(2,1)S(1)} %bitcast.82), kind=kOutput, calls=%fused_computation.5 | convolution fusion | flops 2155872256 | bytes 36700160 | tf_op jit(solution)/shard_map/dot_general | solution.py:53
  356.9 9.6 %fusion.3 = f32[256,2,1024]{0,2,1:T(8,128)} fusion(f32[2,2048,1024]{2,1,0:T(8,128)} %multiply_subtract_fusion, bf16[256,2048]{1,0:T(8,128)(2,1)S(1)} %copy-done), kind=kOutput, calls=%fused_computation.12 | convolution fusion | flops 2151677952 | bytes 19922944 | tf_op jit(solution)/shard_map/bd,pdh->bph/dot_general | solution.py:59
  366.6 2.4 dynamic-slice_bitcast_fusion
  368.9 15.8 %fusion = f32[1,2048,2048]{2,1,0:T(8,128)} fusion(f32[1,2048,2048]{2,1,0:T(8,128)} %param.5, bf16[1,2048,2048]{2,1,0:T(8,128)(2,1)} %param.6, f32[2048,256]{1,0:T(8,128)S(1)} %copy-done.1, bf16[128,2048]{1,0:T(8,128)(2,1)S(1)} %copy-done.4, bf16[128,2048]{1,0:T(8,128)(2,1)S(1)} %copy-done.7), kind=kOutput, calls=%fused_computation.4 | convolution fusion | flops 2166882304 | bytes 45088768 | tf_op jit(solution)/shard_map/dot_general | solution.py:46
  384.8 1.3 fusion.13
  386.1 0.9 copy.26
  (43 shorter events, 0.9 us)
Async XLA Ops:
  7.2 349.8 %copy-start = (bf16[256,2048]{1,0:T(8,128)(2,1)S(1)}, bf16[256,2048]{1,0:T(8,128)(2,1)}, u32[]{:S(2)}) copy-start(bf16[256,2048]{1,0:T(8,128)(2,1)} %param.9) | copy-start | bytes 3145732
  7.2 14.5 %all-gather.5.cloned.1.call-start = ((), (), s32[]{:S(2)}) async-start(), calls=%async_computation.6 | async-start | bytes 1572864 | tf_op jit(solution)/shard_map/all_gather | solution.py:30
  9.4 128.2 %all-reduce.5.cloned.1.call-start = ((), (), s32[]{:S(2)}) async-start(), calls=%async_computation.2 | async-start | bytes 4194304 | tf_op jit(solution)/shard_map/psum | solution.py:33
  33.9 127.7 %all-reduce.7.cloned.1.call-start = ((), (), s32[]{:S(2)}) async-start(), calls=%async_computation.3 | async-start | bytes 524288 | tf_op jit(solution)/shard_map/psum | solution.py:34
  143.9 85.0 %copy-start.2 = (f32[2048,256]{1,0:T(8,128)S(1)}, f32[2048,256]{1,0:T(8,128)}, u32[]{:S(2)}) copy-start(f32[2048,256]{1,0:T(8,128)} %all-reduce.5.cloned.1.call-done) | copy-start | bytes 6291460
  144.0 124.8 %all-reduce.9.cloned.1.call-start = ((), (), s32[]{:S(2)}) async-start(), calls=%async_computation.4 | async-start | bytes 4194304 | tf_op jit(solution)/shard_map/psum | solution.py:40
  163.7 0.7 copy-start.10
  199.9 2.0 copy-start.9
  230.0 2.9 copy-start.5
  232.9 13.2 %copy-start.3 = (bf16[128,2048]{1,0:T(8,128)(2,1)}, bf16[128,2048]{1,0:T(8,128)(2,1)S(1)}, u32[]{:S(2)}) copy-start(bf16[128,2048]{1,0:T(8,128)(2,1)S(1)} %convolution_convert_fusion) | copy-start | bytes 1572868
  246.0 1.0 copy-start.6
  246.1 80.8 %all-gather.7.cloned.1.call-start = ((), (), s32[]{:S(2)}) async-start(), calls=%async_computation.7 | async-start | bytes 3145728 | tf_op jit(solution)/shard_map/all_gather | solution.py:50
  268.7 23.9 %copy-start.1 = (f32[2048,256]{1,0:T(8,128)S(1)}, f32[2048,256]{1,0:T(8,128)}, u32[]{:S(2)}) copy-start(f32[2048,256]{1,0:T(8,128)} %all-reduce.9.cloned.1.call-done) | copy-start | bytes 6291460
  322.3 15.1 %all-to-all-start = ((bf16[2,2,131072]{2,1,0:T(2,128)(2,1)}), bf16[2,2,131072]{2,1,0:T(2,128)(2,1)}, u32[]{:S(2)}, u32[]{:S(2)}) async-start(bf16[2,2,131072]{2,1,0:T(2,128)(2,1)} %reshape.56), calls=%async_computation | async-start | bytes 2097152 | tf_op jit(solution)/shard_map/all_to_all | solution.py:51
  326.8 58.0 %reduce-scatter.2.cloned.1.call-start = ((), (), s32[]{:S(2)}) async-start(), calls=%async_computation.5 | async-start | bytes 3145728 | tf_op jit(solution)/shard_map/reduce_scatter | solution.py:58
  340.4 2.2 copy-start.8
  366.5 2.4 copy-start.4
  366.5 2.4 copy-start.7
Sparse Core Ops, SparseCore 0:
  10.1 11.4 all-gather.4
  34.0 103.4 all-reduce.4
  144.1 17.4 all-reduce.6
  246.2 22.4 all-reduce.8
  270.7 34.2 all-gather.6
  366.7 5.6 reduce-scatter.1
where the time goes:
time: 400 us; the launch traced here: 394 us
  waiting for transfers between devices  160 us (40%)
  matrix products  77.6 us (19%)
  other arithmetic  77.2 us (19%)
  local copies, waits for them, and re-layouts  36.4 us (9%)
  blocking collectives  21.8 us (5%)
  between operations  15.9 us (4%)
  starting transfers between devices  5.19 us (1%)
    psum x1, waiting for transfers between devices, local(): left_full = lax.psum(partial_value, 'col')  104 us
    another operation x6, other arithmetic, orthonormal(): factor_l = jnp.linalg.cholesky(gram_sum)  34 us
    psum x1, blocking collectives, local(): squares = lax.psum(jnp.sum(right_full * right_full, axis=0), 'col')  21.8 us
    another operation x3, other arithmetic, orthonormal(): jax.scipy.linalg.solve_triangular(factor_l, left_rows.T, lower=True)  21.5 us
    psum x1, waiting for transfers between devices, local(): right_full = lax.psum(right_part, 'row')  20.6 us
    psum x1, waiting for transfers between devices, local(): gram_sum = lax.psum(gram_of(left_full), 'row')  17.1 us
    dot_general x1, matrix products, local(): lax.dot_general(left_h, right_h, (((1,), (1,)), ((), ())), preferred_elem...  15.8 us
    dot_general x1, matrix products, local(): lax.dot_general(left_both, right_both, (((2,), (2,)), ((0,), (0,))), pref...  14.3 us
  transfers between devices with their start and end apart: 7, of which 5 were waited for; matrix products, arithmetic and copies ran while one was open for 14% of the time, Pallas kernels for 0%

commit v1 on v0

v1 whole, which is shorter than its diff:
```python
import functools
import math

import jax
import jax.numpy as jnp
from jax import lax
from jax.experimental import pallas as pl
from jax.experimental.pallas import tpu as pltpu
from jax.sharding import PartitionSpec as P


feedback = 0.05
epsilon = 1e-06

f32 = jnp.float32
bf16 = jnp.bfloat16


def peers(n, k):
    return [(i, i ^ k) for i in range(n)]


def bits_of(n):
    assert n & (n - 1) == 0
    return [1 << b for b in range(n.bit_length() - 1)]


def gather_blocks(x, axis, n, at, dim):
    for k in bits_of(n):
        other = lax.ppermute(x, axis, peers(n, k))
        upper = (at & k) != 0
        x = jnp.concatenate([jnp.where(upper, other, x), jnp.where(upper, x, other)], axis=dim)
    return x


def sum_over(x, axis, n, wire=f32):
    for k in bits_of(n):
        x = x + lax.ppermute(x.astype(wire), axis, peers(n, k)).astype(f32)
    return x


def send_all(blocks, axis, n):
    return [lax.ppermute(blocks[k], axis, peers(n, k)) for k in range(1, n)]


def stacked(x, order):
    one = x.astype(bf16)
    rest = x - one.astype(f32)
    two = rest.astype(bf16)
    pieces = (one, two, (rest - two.astype(f32)).astype(bf16))
    return jnp.concatenate([pieces[i] for i in order], axis=0)


def chol_inv_kernel(at_ref, g_ref, out_ref, part_ref, s_ref):
    n = g_ref.shape[0]
    b = 16
    s_ref[:, :n] = g_ref[...]
    s_ref[:, n:] = (
        lax.broadcasted_iota(jnp.int32, (n, n), 0) == lax.broadcasted_iota(jnp.int32, (n, n), 1)
    ).astype(f32)
    rows = lax.broadcasted_iota(jnp.int32, (b, 128), 0)
    for r0 in range(0, n, b):
        lo = r0 // 128 * 128
        hi = n + (r0 + b + 127) // 128 * 128
        tiles = [s_ref[r0 : r0 + b, t : t + 128] for t in range(lo, hi, 128)]
        cols = [
            jnp.broadcast_to(tiles[0][:, r0 - lo + j : r0 - lo + j + 1], (b, 128)) for j in range(b)
        ]
        scale = None
        for i in range(b):
            piv = jnp.broadcast_to(cols[i][i : i + 1, :], (b, 128))
            scale = piv if scale is None else jnp.where(rows == i, piv, scale)
            if i + 1 < b:
                ratio = jnp.where(rows > i, cols[i], 0.0) * (1.0 / piv)
                for j in range(i + 1, b):
                    cols[j] = cols[j] - ratio * cols[j][i : i + 1, :]
                tiles = [t - ratio * t[i : i + 1, :] for t in tiles]
        scale = lax.rsqrt(scale)
        tiles = [t * scale for t in tiles]
        if r0 + b < n:
            upper = jnp.concatenate(tiles, axis=1)
            upd = dot(
                stacked(upper[:, : n - lo], (0, 0, 1, 0, 1, 2)).T,
                stacked(upper, (0, 1, 0, 2, 1, 0)),
            )
            s_ref[r0 + b :, lo:hi] = s_ref[r0 + b :, lo:hi] - upd[r0 + b - lo :, :]
        for k, t in enumerate(range(lo, hi, 128)):
            if t >= n:
                out_ref[r0 : r0 + b, t - n : t - n + 128] = tiles[k]
        for t in range(hi, 2 * n, 128):
            out_ref[r0 : r0 + b, t - n : t - n + 128] = jnp.zeros((b, 128), f32)
    rows = part_ref.shape[0]
    part_ref[...] = out_ref[pl.ds(pl.multiple_of(at_ref[0] * rows, rows), rows), :]


def chol_inv(place, gram, shares):
    n = gram.shape[0]
    return pl.pallas_call(
        chol_inv_kernel,
        out_shape=(pltpu.VMEM((n, n), f32), pltpu.VMEM((n // shares, n), f32)),
        in_specs=[SM, VM],
        out_specs=(VM, VM),
        scratch_shapes=[pltpu.VMEM((n, 2 * n), f32)],
        compiler_params=params(6),
        name="chol_inv",
    )(place, gram)


def split(x):
    hi = x.astype(bf16)
    return hi, (x - hi.astype(f32)).astype(bf16)


def dot_t(a, b):
    return lax.dot_general(a, b, (((1,), (1,)), ((), ())), preferred_element_type=f32)


def dot(a, b):
    return jnp.dot(a, b, preferred_element_type=f32)


VM = pl.BlockSpec(memory_space=pltpu.VMEM)
SM = pl.BlockSpec(memory_space=pltpu.SMEM)
HB = pl.BlockSpec(memory_space=pltpu.HBM)
DMA = pltpu.SemaphoreType.DMA


def params(mib):
    return pltpu.CompilerParams(vmem_limit_bytes=mib << 20)


def rows_per_step(width):
    return min(256, width)


def load_kernel(at_ref, m_ref, g_ref, q_ref, buf_ref, left_ref, grad_ref, sem_m, sem_g):
    width = buf_ref.shape[0]
    _, size, _ = left_ref.shape
    ch = rows_per_step(width)
    copies = []
    for i in range(width // ch):
        at = pl.ds(i * ch, ch)
        pair = (
            pltpu.make_async_copy(m_ref.at[at], buf_ref.at[at], sem_m.at[i]),
            pltpu.make_async_copy(g_ref.at[at], grad_ref.at[at], sem_g.at[i]),
        )
        for c in pair:
            c.start()
        copies.append(pair)
    for i, pair in enumerate(copies):
        at = pl.ds(i * ch, ch)
        for c in pair:
            c.wait()
        buf = buf_ref[at, :] + grad_ref[at, :].astype(f32)
        buf_ref[at, :] = buf
        part = dot(buf.astype(bf16), q_ref[...]).astype(bf16)
        for r in range(0, ch, size):
            left_ref[at_ref[1] ^ ((i * ch + r) // size)] = part[r : r + size, :]


def load_left(place, m, g, q, blocks):
    width, hid = m.shape
    n = width // rows_per_step(width)
    assert rows_per_step(width) % (width // blocks) == 0
    return pl.pallas_call(
        load_kernel,
        out_shape=(
            pltpu.VMEM((width, hid), f32),
            pltpu.VMEM((blocks, width // blocks, q.shape[1]), bf16),
        ),
        in_specs=[SM, HB, HB, VM],
        out_specs=(VM, VM),
        scratch_shapes=[pltpu.VMEM((width, hid), bf16), DMA((n,)), DMA((n,))],
        compiler_params=params(16),
        name="load_left",
    )(place, in_hbm(m), in_hbm(g), q)


def in_hbm(x):
    return pltpu.with_memory_space_constraint(x, pltpu.HBM)


def fetch_kernel(at_ref, w_ref, after_ref, out_ref, sem):
    copies = []
    ch = rows_per_step(w_ref.shape[1])
    for i in range(w_ref.shape[1] // ch):
        at = pl.ds(i * ch, ch)
        copies.append(
            pltpu.make_async_copy(w_ref.at[at_ref[2], at], out_ref.at[at], sem.at[i])
        )
    for c in copies:
        c.start()
    for c in copies:
        c.wait()


def fetch(place, w, after):
    n = w.shape[1] // rows_per_step(w.shape[1])
    return pl.pallas_call(
        fetch_kernel,
        out_shape=pltpu.VMEM(w.shape[1:], w.dtype),
        in_specs=[SM, HB, VM],
        out_specs=VM,
        scratch_shapes=[DMA((n,))],
        compiler_params=params(1),
        name="fetch_weights",
    )(place, w, after)


def sum_kernel(*refs):
    total = refs[0][...].astype(f32)
    for r in refs[1:-1]:
        total = total + r[...].astype(f32)
    refs[-1][...] = total.astype(bf16)


def block_sum(blocks):
    return pl.pallas_call(
        sum_kernel,
        out_shape=pltpu.VMEM(blocks[0].shape, bf16),
        in_specs=[VM] * len(blocks),
        out_specs=VM,
        compiler_params=params(4),
        name="block_sum",
    )(*blocks)


def gram_kernel(at_ref, *refs):
    blocks, raw_ref, gram_ref = refs[:-2], refs[-2], refs[-1]
    size = blocks[0].shape[0]
    for k, r in enumerate(blocks):
        start = pl.multiple_of((at_ref[1] ^ k) * size, size)
        raw_ref[pl.ds(start, size), :] = r[...]
    raw = raw_ref[...]
    gram_ref[...] = lax.dot_general(
        raw, raw, (((0,), (0,)), ((), ())), preferred_element_type=f32
    )


def join_gram(place, blocks):
    size, rank = blocks[0].shape
    return pl.pallas_call(
        gram_kernel,
        out_shape=(pltpu.VMEM((size * len(blocks), rank), bf16), pltpu.VMEM((rank, rank), f32)),
        in_specs=[SM] + [VM] * len(blocks),
        out_specs=(VM, VM),
        compiler_params=params(6),
        name="join_gram",
    )(place, *blocks)


def right_kernel(raw_ref, buf_ref, out_ref, outh_ref):
    raw_t = raw_ref[...].T
    hid = buf_ref.shape[1]
    ch = min(256, hid)
    for i in range(hid // ch):
        at = pl.ds(i * ch, ch)
        part = dot(raw_t, buf_ref[:, at].astype(bf16))
        out_ref[:, at] = part
        outh_ref[:, at] = part.astype(bf16)


def raw_right(raw, buf):
    shape = (raw.shape[1], buf.shape[1])
    return pl.pallas_call(
        right_kernel,
        out_shape=(pltpu.VMEM(shape, f32), pltpu.VMEM(shape, bf16)),
        in_specs=[VM, VM],
        out_specs=(VM, VM),
        compiler_params=params(6),
        name="raw_right",
    )(raw, buf)


def factors_kernel(
    at_ref, raw_ref, inv_ref, rr_ref, rro_ref, left_ref, right_ref, righth_ref, own_ref, part_ref, sq_ref,
    split_ref,
):
    inv_hi, inv_lo = split(inv_ref[...])
    left_ref[...] = (dot_t(raw_ref[...], inv_hi) + dot_t(raw_ref[...], inv_lo)).astype(bf16)
    hid = rr_ref.shape[1]
    half = split_ref.shape[2]
    ch = min(512, half)
    total = jnp.zeros((rr_ref.shape[0], 1), f32)
    for i in range(hid // ch):
        at = pl.ds(i * ch, ch)
        hi, lo = split(rr_ref[:, at] + rro_ref[:, at].astype(f32))
        right = dot(inv_hi, hi) + dot(inv_lo, hi) + dot(inv_hi, lo)
        right_ref[:, at] = right
        right_h = right.astype(bf16)
        righth_ref[:, at] = right_h
        split_ref[at_ref[2] ^ (i * ch // half), :, pl.ds(i * ch % half, ch)] = right_h
        total = total + jnp.sum(right * right, axis=1, keepdims=True)
    own_ref[...] = split_ref[0]
    rows = part_ref.shape[0]
    part_ref[...] = split_ref[1, pl.ds(pl.multiple_of(at_ref[0] * rows, rows), rows), :]
    sq_ref[...] = jnp.broadcast_to(total, (total.shape[0], 128)).T[: sq_ref.shape[0], :]


def factors(place, raw, inv_l, rr, rro, groups, shares):
    rank, hid = rr.shape
    return pl.pallas_call(
        factors_kernel,
        out_shape=(
            pltpu.VMEM(raw.shape, bf16),
            pltpu.VMEM((rank, hid), f32),
            pltpu.VMEM((rank, hid), bf16),
            pltpu.VMEM((rank, hid // groups), bf16),
            pltpu.VMEM((rank // shares, hid // groups), bf16),
            pltpu.VMEM((8, rank), f32),
        ),
        in_specs=[SM, VM, VM, VM, VM],
        out_specs=(VM, VM, VM, VM, VM, VM),
        scratch_shapes=[pltpu.VMEM((groups, rank, hid // groups), bf16)],
        compiler_params=params(6),
        name="factors",
    )(place, raw, inv_l, rr, rro)


def share_kernel(at_ref, right_ref, norm_ref, out_ref, col_ref):
    n = out_ref.shape[1]
    col_ref[...] = norm_ref[...].T
    at = pl.ds(pl.multiple_of(at_ref[0] * n, n), n)
    out_ref[...] = (right_ref[at, :] * col_ref[at, 0:1]).T


def factor_share(place, right, inv_norm, share):
    rank, hid = right.shape
    return pl.pallas_call(
        share_kernel,
        out_shape=jax.ShapeDtypeStruct((hid, share), f32),
        in_specs=[SM, VM, VM],
        out_specs=VM,
        scratch_shapes=[pltpu.VMEM((rank, 8), f32)],
        compiler_params=params(6),
        name="factor_share",
    )(place, right, inv_norm)


SLOTS = 4


def feedback_kernel(buf_ref, left_ref, right_ref, *rest, lo, hi, ch):
    out_ref, stage_ref, sem = rest[-3:]
    pending = []
    for i, r in enumerate(range(lo, hi, ch)):
        slot = i % SLOTS
        if i >= SLOTS:
            pending[i - SLOTS].wait()
        at = pl.ds(r, ch)
        stage_ref[slot] = buf_ref[at, :] - feedback * dot(left_ref[at, :], right_ref[...])
        copy = pltpu.make_async_copy(stage_ref.at[slot], out_ref.at[at], sem.at[slot])
        copy.start()
        pending.append(copy)
    for copy in pending[-SLOTS:]:
        copy.wait()


def apply_feedback(buf, left, right, out, lo, hi):
    width, hid = buf.shape
    ch = min(128, hi - lo)
    args = (buf, left, right) + (() if out is None else (out,))
    return pl.pallas_call(
        functools.partial(feedback_kernel, lo=lo, hi=hi, ch=ch),
        out_shape=pltpu.HBM((width, hid), f32),
        in_specs=[VM, VM, VM] + ([] if out is None else [HB]),
        out_specs=HB,
        input_output_aliases={} if out is None else {3: 0},
        scratch_shapes=[pltpu.VMEM((SLOTS, ch, hid), f32), DMA((SLOTS,))],
        compiler_params=params(8),
        name="feedback",
    )(*args)


WSLOTS = 4


def update_kernel(at_ref, w_ref, raw_ref, scale_ref, tok_ref, *rest, other, shares):
    n = shares if other else 1
    if other:
        rest, near_ref, wsem = rest[:-2], rest[-2], rest[-1]
    invs, rights = rest[:n], rest[n : 2 * n]
    out_ref, decs = rest[-6 - shares], rest[-5 - shares : -5]
    inv_ref, right_ref, stage_ref, acc_ref, sem = rest[-5:]
    width = raw_ref.shape[0]
    ch = rows_per_step(width)
    p = at_ref[2] ^ other
    reads = []
    if other:
        for i, r in enumerate(range(0, width, ch)):
            at = pl.ds(r, ch)
            reads.append(pltpu.make_async_copy(w_ref.at[p, at], near_ref.at[at], wsem.at[i]))
            reads[-1].start()
        w_ref = near_ref
    for j in range(n):
        rows = invs[j].shape[0]
        at = pl.ds(pl.multiple_of((at_ref[0] ^ j) * rows, rows), rows) if other else slice(None)
        inv_ref[at, :] = invs[j][...]
        right_ref[at, :] = rights[j][...]
    pending = []
    share = decs[0].shape[0]
    hi, lo = split(inv_ref[...])
    scale = scale_ref[0:1, :]
    right = right_ref[...]
    acc = None
    for r in range(0, width, ch):
        at = pl.ds(r, ch)
        slot = len(pending) % WSLOTS
        if len(pending) >= WSLOTS:
            pending[len(pending) - WSLOTS].wait()
        raw = raw_ref[at, :]
        left = ((dot_t(raw, hi) + dot_t(raw, lo)) * scale).astype(bf16)
        if other:
            reads[r // ch].wait()
        new = w_ref[at, :] - dot(left, right)
        stage_ref[slot] = new
        copy = pltpu.make_async_copy(stage_ref.at[slot], out_ref.at[p, at], sem.at[slot])
        copy.start()
        pending.append(copy)
        part = dot(tok_ref[:, at], new.astype(bf16))
        acc = part if acc is None else acc + part
    acc_ref[...] = acc
    for j, dec in enumerate(decs):
        dec[...] = acc_ref[pl.ds(pl.multiple_of((at_ref[0] ^ j) * share, share), share), :]
    for copy in pending[-WSLOTS:]:
        copy.wait()


def update(place, w, raw, scale, tokens, invs, rights, out, shares):
    width, half = w.shape[-2:]
    rank = raw.shape[1]
    ch = rows_per_step(width)
    other = out is not None
    args = (place, w, raw, scale, tokens, *invs, *rights) + ((out,) if other else ())
    batch = tokens.shape[0]
    new, *decs = pl.pallas_call(
        functools.partial(update_kernel, other=int(other), shares=shares),
        out_shape=(pltpu.HBM((2, width, half), f32),)
        + (pltpu.VMEM((batch // shares, half), f32),) * shares,
        in_specs=[SM, HB if other else VM]
        + [VM] * (3 + len(invs) + len(rights))
        + ([HB] if other else []),
        out_specs=(HB,) + (VM,) * shares,
        input_output_aliases={len(args) - 1: 0} if other else {},
        scratch_shapes=[
            pltpu.VMEM((rank, rank), f32),
            pltpu.VMEM((rank, half), bf16),
            pltpu.VMEM((WSLOTS, ch, half), f32),
            pltpu.VMEM((batch, half), f32),
            DMA((WSLOTS,)),
        ]
        + ([pltpu.VMEM((width, half), f32), DMA((width // ch,))] if other else []),
        compiler_params=params(18 if other else 9),
        name="update_other" if other else "update_own",
    )(*args)
    return new, decs


def finish_kernel(at_ref, *refs):
    n = (len(refs) - 1) // 2
    own, other = refs[0][...], refs[n][...]
    for k in range(1, n):
        own = own + refs[k][...]
        other = other + refs[n + k][...]
    first = at_ref[2] == 0
    gate, up = jnp.where(first, own, other), jnp.where(first, other, own)
    refs[-1][...] = (gate / (1.0 + jnp.exp(-gate)) * up).astype(bf16)


def finish(place, own, other):
    return pl.pallas_call(
        finish_kernel,
        out_shape=jax.ShapeDtypeStruct(own[0].shape, bf16),
        in_specs=[SM] + [VM] * (len(own) + len(other)),
        out_specs=VM,
        compiler_params=params(4),
        name="finish",
    )(place, *own, *other)


def make_local(nrow, ncol, ngrp):
    def local(momentum, gradient, factor_q, weights, tokens):
        return step(momentum, gradient, factor_q, weights, tokens)

    def step(momentum, gradient, factor_q, weights, tokens):
        row = lax.axis_index("row")
        place = jnp.stack([row, lax.axis_index("col"), lax.axis_index("grp")]).astype(jnp.int32)
        width, hid = momentum.shape[1], momentum.shape[2]
        swap = peers(ngrp, 1)
        q_h = gather_blocks(factor_q[0].astype(bf16), "row", nrow, row, 1)
        buffer, parts = load_left(place, momentum[0], gradient[0], q_h, ncol)
        parts = [parts[k] for k in range(ncol)]
        got = send_all(parts, "col", ncol)
        weights = in_hbm(weights)
        w_own = fetch(place, weights, parts[0])
        block = block_sum([parts[0]] + got)
        raw, gram = join_gram(place, [block] + send_all([block] * ncol, "col", ncol))
        raw_other = lax.ppermute(raw, "grp", swap)
        gram = sum_over(gram, "row", nrow)
        rr, rr_h = raw_right(raw, buffer)
        for k in bits_of(nrow)[:-1]:
            rr = rr + lax.ppermute(rr_h, "row", peers(nrow, k)).astype(f32)
            rr_h = rr.astype(bf16)
        rr_other = lax.ppermute(rr_h, "row", peers(nrow, bits_of(nrow)[-1]))
        inv_l, inv_part = chol_inv(place, gram, nrow)
        inv_part = lax.ppermute(inv_part, "grp", swap)
        left_h, right, right_h, right_own, half_part, squares = factors(
            place, raw, inv_l, rr, rr_other, ngrp, nrow
        )
        half_part = lax.ppermute(half_part, "grp", swap)
        rounds = bits_of(ncol)
        cuts = [width * i // 4 for i in range(5)]
        mom_new = None
        for i in range(4):
            mom_new = apply_feedback(buffer, left_h, right_h, mom_new, cuts[i], cuts[i + 1])
        for k in rounds:
            squares = squares + lax.ppermute(squares, "col", peers(ncol, k))
        step_size = 0.4 * math.sqrt(max(width * nrow, hid * ncol))
        inv_norm = 1.0 / jnp.sqrt(squares + epsilon)
        inv_norm_other = lax.ppermute(inv_norm, "grp", swap)
        q_share = factor_share(place, right, inv_norm, factor_q.shape[2])
        scale, mom_new = lax.optimization_barrier((step_size * inv_norm, mom_new))
        new_weights, dec = update(
            place, w_own, raw, scale, tokens, [inv_l], [right_own], None, nrow
        )
        inv_part, half_part, mom_new = lax.optimization_barrier(
            (inv_part, half_part, mom_new)
        )
        invs = [inv_part] + send_all([inv_part] * nrow, "row", nrow)
        halves = [half_part] + send_all([half_part] * nrow, "row", nrow)
        new_weights, dec_other = update(
            place, weights, raw_other, step_size * inv_norm_other, tokens, invs, halves,
            new_weights, nrow,
        )
        dec[1:] = send_all(dec, "row", nrow)
        dec_other[1:] = send_all(dec_other, "row", nrow)
        hidden = finish(place, dec, dec_other)
        return (mom_new[None], q_share[None], new_weights, hidden)

    return local


def solution(mesh):
    in_specs = (
        P("grp", "row", "col"),
        P("grp", "row", "col"),
        P("grp", "col", "row"),
        P(None, "row", ("col", "grp")),
        P(None, "row"),
    )
    out_specs = (
        P("grp", "row", "col"),
        P("grp", "col", "row"),
        P(None, "row", ("col", "grp")),
        P("row", ("col", "grp")),
    )
    local = make_local(mesh.shape["row"], mesh.shape["col"], mesh.shape["grp"])
    return jax.shard_map(local, mesh=mesh, in_specs=in_specs, out_specs=out_specs, check_vma=False)
```

time: 400 us -> 138 us (0.34); the launches traced: 394 us -> 138 us
  waiting for transfers between devices: 160 us -> 34.7 us
  matrix products: 77.6 us -> 0 us
  other arithmetic: 77.2 us -> 2.85 us
  Pallas kernels: 0 us -> 55.8 us
  starting transfers between devices: 5.19 us -> 43.4 us
  local copies, waits for them, and re-layouts: 36.4 us -> 0.08 us
  blocking collectives: 21.8 us -> 0 us
  between operations: 15.9 us -> 0.84 us
    psum x3 -> x0, waiting for transfers between devices: 141 us -> none  [the longest x1 104 us: local(): left_full = lax.psum(partial_value, 'col')]
    dot_general x6 -> x0, matrix products: 71.5 us -> none  [the longest x1 15.8 us: local(): lax.dot_general(left_h, right_h, (((1,), (1,)), ((), ())), preferred_elem...]
    pallas_call x0 -> x15, Pallas kernels: none -> 55.8 us  [the longest x2 14.9 us: update(): pl.pallas_call(functools.partial(update_kernel, other=int(other), shares=...]
    another operation x9 -> x1, other arithmetic: 55.5 us -> 0.08 us  [step(): jnp.stack([row, lax.axis_index('col'), lax.axis_index('grp')])]
    ppermute x0 -> x28, starting transfers between devices: none -> 43.4 us  [the longest x18 28.5 us: send_all(): return [lax.ppermute(blocks[k], axis, peers(n, k)) for k in range(1, n)]]
    ppermute x0 -> x28, waiting for transfers between devices: none -> 34.7 us  [the longest x18 28.6 us: send_all(): return [lax.ppermute(blocks[k], axis, peers(n, k)) for k in range(1, n)]]
    psum x1 -> x0, blocking collectives: 21.8 us -> none  [local(): squares = lax.psum(jnp.sum(right_full * right_full, axis=0), 'col')]
    broadcast_in_dim x2 -> x0, local copies, waits for them, and re-layouts: 15.2 us -> none  [the longest x1 12.9 us: local(): new_q_h[None]]
  transfers between devices with their start and end apart: 7 -> 28, of which waited for: 5 -> 11; matrix products, arithmetic and copies ran while one was open for 14% -> 0% of each run, Pallas kernels for 0% -> 30%
where the time goes in v1:
time: 138 us
  Pallas kernels  55.8 us (40%)
  starting transfers between devices  43.4 us (31%)
  waiting for transfers between devices  34.7 us (25%)
  other arithmetic  2.85 us (2%)
    ppermute x18, waiting for transfers between devices, send_all(): return [lax.ppermute(blocks[k], axis, peers(n, k)) for k in range(1, n)]  28.6 us
    ppermute x18, starting transfers between devices, send_all(): return [lax.ppermute(blocks[k], axis, peers(n, k)) for k in range(1, n)]  28.5 us
    pallas_call x2, Pallas kernels, update(): pl.pallas_call(functools.partial(update_kernel, other=int(other), shares=...  14.9 us
    pallas_call x1, Pallas kernels, load_left(): pl.pallas_call(load_kernel, out_shape=(pltpu.VMEM((width, hid), f32), plt...  9.57 us
    pallas_call x4, Pallas kernels, apply_feedback(): pl.pallas_call(functools.partial(feedback_kernel, lo=lo, hi=hi, ch=ch), o...  9.53 us
    ppermute x3, starting transfers between devices, step(): squares = squares + lax.ppermute(squares, 'col', peers(ncol, k))  9.03 us
    pallas_call x1, Pallas kernels, chol_inv(): pl.pallas_call(chol_inv_kernel, out_shape=(pltpu.VMEM((n, n), f32), pltpu...  8.13 us
    pallas_call x1, Pallas kernels, fetch(): pl.pallas_call(fetch_kernel, out_shape=pltpu.VMEM(w.shape[1:], w.dtype),...  4.02 us
  transfers between devices with their start and end apart: 28, of which 11 were waited for; matrix products, arithmetic and copies ran while one was open for 0% of the time, Pallas kernels for 30%

profile of v1, /device:TPU:0, one launch (start us, length us, event | category | flops | bytes accessed | tf_op | source)
XLA Modules:
  0.0 137.7 jit_solution(6273856732342262581)
XLA Ops:
  0.6 1.3 convert_bitcast_fusion
  1.9 0.6 collective-permute-start
  2.5 1.5 %collective-permute-done = bf16[2048,128]{1,0:T(8,128)(2,1)S(1)} collective-permute-done((bf16[2048,128]{1,0:T(8,128)(2,1)S(1)}, bf16[2048,128]{1,0:T(8,128)(2,1)S(1)}, u32[]{:S(2)}, u32[]{:S(2)}) %collective-permute-start) | collective-permute-done | bytes 524320 | tf_op jit(solution)/shard_map/ppermute | solution.py:30
  4.0 1.3 broadcast_select_fusion.1
  5.5 9.6 %load_left.1 = (f32[2048,2048]{1,0:T(8,128)S(1)}, bf16[8,256,256]{2,1,0:T(8,128)(2,1)S(1)}) custom-call(s32[3]{0:T(128)S(1)} %pad_add_fusion.at_ref, f32[2048,2048]{1,0:T(8,128)} %bitcast.28, bf16[2048,2048]{1,0:T(8,128)(2,1)} %bitcast.29, bf16[2048,256]{1,0:T(8,128)(2,1)S(1)} %pad_maximum_fusion.q_ref), custom_call_target="tpu_custom_call" | custom-call | tf_op jit(solution)/shard_map/load_left/pallas_call | solution.py:165
  15.1 2.9 %collective-permute-start.1 = (bf16[256,256]{1,0:T(8,128)(2,1)S(1)}, bf16[256,256]{1,0:T(8,128)(2,1)S(1)}, u32[]{:S(2)}, u32[]{:S(2)}) collective-permute-start(bf16[256,256]{1,0:T(8,128)(2,1)S(1)} %get-tuple-element.62), channel_id=1, source_target_pairs={{0,2},{2,0},{4,6},{6,4},{8,10},{10,8},{12,14},{14,12},{1,3},{3,1},... | collective-permute-start | bytes 393224 | tf_op jit(solution)/shard_map/ppermute | solution.py:43
  18.0 1.6 %collective-permute-start.2 = (bf16[256,256]{1,0:T(8,128)(2,1)S(1)}, bf16[256,256]{1,0:T(8,128)(2,1)S(1)}, u32[]{:S(2)}, u32[]{:S(2)}) collective-permute-start(bf16[256,256]{1,0:T(8,128)(2,1)S(1)} %get-tuple-element.61), channel_id=1, source_target_pairs={{0,4},{2,6},{4,0},{6,2},{8,12},{10,14},{12,8},{14,10},{1,5},{3,7},... | collective-permute-start | bytes 393224 | tf_op jit(solution)/shard_map/ppermute | solution.py:43
  19.6 3.0 %collective-permute-start.4 = (bf16[256,256]{1,0:T(8,128)(2,1)S(1)}, bf16[256,256]{1,0:T(8,128)(2,1)S(1)}, u32[]{:S(2)}, u32[]{:S(2)}) collective-permute-start(bf16[256,256]{1,0:T(8,128)(2,1)S(1)} %get-tuple-element.59), channel_id=1, source_target_pairs={{0,8},{2,10},{4,12},{6,14},{8,0},{10,2},{12,4},{14,6},{1,9},{3,11}... | collective-permute-start | bytes 393224 | tf_op jit(solution)/shard_map/ppermute | solution.py:43
  22.6 1.3 collective-permute-start.5
  23.9 3.6 %collective-permute-start.6 = (bf16[256,256]{1,0:T(8,128)(2,1)S(1)}, bf16[256,256]{1,0:T(8,128)(2,1)S(1)}, u32[]{:S(2)}, u32[]{:S(2)}) collective-permute-start(bf16[256,256]{1,0:T(8,128)(2,1)S(1)} %get-tuple-element.57), channel_id=1, source_target_pairs={{0,12},{2,14},{4,8},{6,10},{8,4},{10,6},{12,0},{14,2},{1,13},{3,15... | collective-permute-start | bytes 393224 | tf_op jit(solution)/shard_map/ppermute | solution.py:43
  27.5 1.3 collective-permute-done.2.refs_2_
  28.8 0.7 collective-permute-start.7
  29.5 0.6 collective-permute-done.3.refs_3_
  30.1 11.6 %collective-permute-done.5.refs_5_ = bf16[256,256]{1,0:T(8,128)(2,1)S(1)} collective-permute-done((bf16[256,256]{1,0:T(8,128)(2,1)S(1)}, bf16[256,256]{1,0:T(8,128)(2,1)S(1)}, u32[]{:S(2)}, u32[]{:S(2)}) %collective-permute-start.5) | collective-permute-done | bytes 131104 | tf_op jit(solution)/shard_map/ppermute | solution.py:43
  41.8 5.6 %collective-permute-start.10 = (bf16[256,256]{1,0:T(8,128)(2,1)S(1)}, bf16[256,256]{1,0:T(8,128)(2,1)S(1)}, u32[]{:S(2)}, u32[]{:S(2)}) collective-permute-start(bf16[256,256]{1,0:T(8,128)(2,1)S(1)} %block_sum.1.refs_0_), channel_id=1, source_target_pairs={{0,6},{2,4},{4,2},{6,0},{8,14},{10,12},{12,10},{14,8},{1,7},{3,5},... | collective-permute-start | bytes 393224 | tf_op jit(solution)/shard_map/ppermute | solution.py:43
  47.4 1.9 %collective-permute-start.11 = (bf16[256,256]{1,0:T(8,128)(2,1)S(1)}, bf16[256,256]{1,0:T(8,128)(2,1)S(1)}, u32[]{:S(2)}, u32[]{:S(2)}) collective-permute-start(bf16[256,256]{1,0:T(8,128)(2,1)S(1)} %block_sum.1.refs_0_), channel_id=1, source_target_pairs={{0,8},{2,10},{4,12},{6,14},{8,0},{10,2},{12,4},{14,6},{1,9},{3,11}... | collective-permute-start | bytes 393224 | tf_op jit(solution)/shard_map/ppermute | solution.py:43
  49.2 1.8 %collective-permute-start.12 = (bf16[256,256]{1,0:T(8,128)(2,1)S(1)}, bf16[256,256]{1,0:T(8,128)(2,1)S(1)}, u32[]{:S(2)}, u32[]{:S(2)}) collective-permute-start(bf16[256,256]{1,0:T(8,128)(2,1)S(1)} %block_sum.1.refs_0_), channel_id=1, source_target_pairs={{0,10},{2,8},{4,14},{6,12},{8,2},{10,0},{12,6},{14,4},{1,11},{3,9}... | collective-permute-start | bytes 393224 | tf_op jit(solution)/shard_map/ppermute | solution.py:43
  51.1 3.4 %collective-permute-start.13 = (bf16[256,256]{1,0:T(8,128)(2,1)S(1)}, bf16[256,256]{1,0:T(8,128)(2,1)S(1)}, u32[]{:S(2)}, u32[]{:S(2)}) collective-permute-start(bf16[256,256]{1,0:T(8,128)(2,1)S(1)} %block_sum.1.refs_0_), channel_id=1, source_target_pairs={{0,12},{2,14},{4,8},{6,10},{8,4},{10,6},{12,0},{14,2},{1,13},{3,15... | collective-permute-start | bytes 393224 | tf_op jit(solution)/shard_map/ppermute | solution.py:43
  54.4 0.6 collective-permute-start.14
  55.0 1.3 collective-permute-start.8
  56.4 8.5 %collective-permute-done.11.refs_4_ = bf16[256,256]{1,0:T(8,128)(2,1)S(1)} collective-permute-done((bf16[256,256]{1,0:T(8,128)(2,1)S(1)}, bf16[256,256]{1,0:T(8,128)(2,1)S(1)}, u32[]{:S(2)}, u32[]{:S(2)}) %collective-permute-start.11) | collective-permute-done | bytes 131104 | tf_op jit(solution)/shard_map/ppermute | solution.py:43
  64.9 4.4 %collective-permute-done.12.refs_5_ = bf16[256,256]{1,0:T(8,128)(2,1)S(1)} collective-permute-done((bf16[256,256]{1,0:T(8,128)(2,1)S(1)}, bf16[256,256]{1,0:T(8,128)(2,1)S(1)}, u32[]{:S(2)}, u32[]{:S(2)}) %collective-permute-start.12) | collective-permute-done | bytes 131104 | tf_op jit(solution)/shard_map/ppermute | solution.py:43
  69.3 0.6 collective-permute-done.9.refs_2_
  69.9 1.1 join_gram.1
  71.0 2.5 %raw_right.1 = (f32[256,2048]{1,0:T(8,128)S(1)}, bf16[256,2048]{1,0:T(8,128)(2,1)S(1)}) custom-call(bf16[2048,256]{1,0:T(8,128)(2,1)S(1)} %get-tuple-element.32.raw_ref, f32[2048,2048]{1,0:T(8,128)S(1)} %get-tuple-element.34.buf_ref), custom_call_target="tpu_custom_call" | custom-call | tf_op jit(solution)/shard_map/raw_right/pallas_call | solution.py:265
  73.6 1.6 %collective-permute-start.22 = (bf16[2048,256]{1,0:T(8,128)(2,1)S(1)}, bf16[2048,256]{1,0:T(8,128)(2,1)S(1)}, u32[]{:S(2)}, u32[]{:S(2)}) collective-permute-start(bf16[2048,256]{1,0:T(8,128)(2,1)S(1)} %get-tuple-element.32.raw_ref), channel_id=1, source_target_pairs={{0,1},{1,0},{2,3},{3,2},{4,5},{5,4},{6,7},{7,6},{8,9},{9,8},{10,11... | collective-permute-start | bytes 3145736 | tf_op jit(solution)/shard_map/ppermute | solution.py:498
  75.3 1.4 %collective-permute-done.15 = f32[256,256]{1,0:T(8,128)S(1)} collective-permute-done((f32[256,256]{1,0:T(8,128)S(1)}, f32[256,256]{1,0:T(8,128)S(1)}, u32[]{:S(2)}, u32[]{:S(2)}) %collective-permute-start.15) | collective-permute-done | bytes 262176 | tf_op jit(solution)/shard_map/ppermute | solution.py:38
  76.7 8.1 %chol_inv.1 = (f32[256,256]{1,0:T(8,128)S(1)}, f32[128,256]{1,0:T(8,128)S(1)}) custom-call(s32[3]{0:T(128)S(1)} %pad_add_fusion.at_ref, f32[256,256]{1,0:T(8,128)S(1)} %add.18.g_ref), custom_call_target="tpu_custom_call" | custom-call | tf_op jit(solution)/shard_map/chol_inv/pallas_call | solution.py:98
  84.9 2.4 %factors.1 = (bf16[2048,256]{1,0:T(8,128)(2,1)S(1)}, f32[256,2048]{1,0:T(8,128)S(1)}, bf16[256,2048]{1,0:T(8,128)(2,1)S(1)}, bf16[256,1024]{1,0:T(8,128)(2,1)S(1...) custom-call(s32[3]{0:T(128)S(1)} %pad_add_fusion.at_ref, bf16[2048,256]{1,0:T(8,128)(2,1)S(1)} %get-tuple-element.32.raw_ref, ...), custom_call_target="tpu_custom_call" | custom-call | tf_op jit(solution)/shard_map/factors/pallas_call | solution.py:302
  87.3 1.5 %collective-permute-start.18 = (bf16[128,1024]{1,0:T(8,128)(2,1)S(1)}, bf16[128,1024]{1,0:T(8,128)(2,1)S(1)}, u32[]{:S(2)}, u32[]{:S(2)}) collective-permute-start(bf16[128,1024]{1,0:T(8,128)(2,1)S(1)} %get-tuple-element.37), channel_id=1, source_target_pairs={{0,1},{1,0},{2,3},{3,2},{4,5},{5,4},{6,7},{7,6},{8,9},{9,8},{10,11... | collective-permute-start | bytes 786440 | tf_op jit(solution)/shard_map/ppermute | solution.py:510
  88.7 2.1 %collective-permute-start.19 = (f32[8,256]{1,0:T(8,128)S(1)}, f32[8,256]{1,0:T(8,128)S(1)}, u32[]{:S(2)}, u32[]{:S(2)}) collective-permute-start(f32[8,256]{1,0:T(8,128)S(1)} %get-tuple-element.38), channel_id=1, source_target_pairs={{0,2},{2,0},{4,6},{6,4},{8,10},{10,8},{12,14},{14,12},{1,3},{3,1},... | collective-permute-start | bytes 24584 | tf_op jit(solution)/shard_map/ppermute | solution.py:517
  90.8 1.6 %collective-permute-done.19 = f32[8,256]{1,0:T(8,128)S(1)} collective-permute-done((f32[8,256]{1,0:T(8,128)S(1)}, f32[8,256]{1,0:T(8,128)S(1)}, u32[]{:S(2)}, u32[]{:S(2)}) %collective-permute-start.19) | collective-permute-done | bytes 8224 | tf_op jit(solution)/shard_map/ppermute | solution.py:517
  92.5 3.9 %collective-permute-start.20 = (f32[8,256]{1,0:T(8,128)S(1)}, f32[8,256]{1,0:T(8,128)S(1)}, u32[]{:S(2)}, u32[]{:S(2)}) collective-permute-start(f32[8,256]{1,0:T(8,128)S(1)} %add.19), channel_id=1, source_target_pairs={{0,4},{2,6},{4,0},{6,2},{8,12},{10,14},{12,8},{14,10},{1,5},{3,7},... | collective-permute-start | bytes 24584 | tf_op jit(solution)/shard_map/ppermute | solution.py:517
  96.3 1.6 %collective-permute-done.20 = f32[8,256]{1,0:T(8,128)S(1)} collective-permute-done((f32[8,256]{1,0:T(8,128)S(1)}, f32[8,256]{1,0:T(8,128)S(1)}, u32[]{:S(2)}, u32[]{:S(2)}) %collective-permute-start.20) | collective-permute-done | bytes 8224 | tf_op jit(solution)/shard_map/ppermute | solution.py:517
  97.9 3.1 %collective-permute-start.21 = (f32[8,256]{1,0:T(8,128)S(1)}, f32[8,256]{1,0:T(8,128)S(1)}, u32[]{:S(2)}, u32[]{:S(2)}) collective-permute-start(f32[8,256]{1,0:T(8,128)S(1)} %add.20), channel_id=1, source_target_pairs={{0,8},{2,10},{4,12},{6,14},{8,0},{10,2},{12,4},{14,6},{1,9},{3,11}... | collective-permute-start | bytes 24584 | tf_op jit(solution)/shard_map/ppermute | solution.py:517
  101.0 0.6 collective-permute-start.16
  101.6 2.4 %feedback.4.rest_0_ = f32[2048,2048]{1,0:T(8,128)} custom-call(f32[2048,2048]{1,0:T(8,128)S(1)} %get-tuple-element.34.buf_ref, bf16[2048,256]{1,0:T(8,128)(2,1)S(1)} %get-tuple-element.39.left_ref, bf16[256,2048]{1,0:T(8,128)(2,1)S(1)} %get-tuple-element.40.right_ref), custom_call_target="tpu_custom_call" | custom-call | tf_op jit(solution)/shard_map/feedback/pallas_call | solution.py:363
  104.0 2.4 %feedback.5.rest_0_ = f32[2048,2048]{1,0:T(8,128)} custom-call(f32[2048,2048]{1,0:T(8,128)S(1)} %get-tuple-element.34.buf_ref, bf16[2048,256]{1,0:T(8,128)(2,1)S(1)} %get-tuple-element.39.left_ref, bf16[256,2048]{1,0:T(8,128)(2,1)S(1)} %get-tuple-element.40.right_ref, f32[2048,2048]{1,0:T(8,128)} %feedback.4.rest_0_), custom_call_target="tpu_custom_call", output_to_operand_aliasing={{}: (3, {})} | custom-call | tf_op jit(solution)/shard_map/feedback/pallas_call | solution.py:363
  106.4 2.4 %feedback.6.rest_0_ = f32[2048,2048]{1,0:T(8,128)} custom-call(f32[2048,2048]{1,0:T(8,128)S(1)} %get-tuple-element.34.buf_ref, bf16[2048,256]{1,0:T(8,128)(2,1)S(1)} %get-tuple-element.39.left_ref, bf16[256,2048]{1,0:T(8,128)(2,1)S(1)} %get-tuple-element.40.right_ref, f32[2048,2048]{1,0:T(8,128)} %feedback.5.rest_0_), custom_call_target="tpu_custom_call", output_to_operand_aliasing={{}: (3, {})} | custom-call | tf_op jit(solution)/shard_map/feedback/pallas_call | solution.py:363
  108.8 2.4 %feedback.7 = f32[2048,2048]{1,0:T(8,128)} custom-call(f32[2048,2048]{1,0:T(8,128)S(1)} %get-tuple-element.34.buf_ref, bf16[2048,256]{1,0:T(8,128)(2,1)S(1)} %get-tuple-element.39.left_ref, bf16[256,2048]{1,0:T(8,128)(2,1)S(1)} %get-tuple-element.40.right_ref, f32[2048,2048]{1,0:T(8,128)} %feedback.6.rest_0_), custom_call_target="tpu_custom_call", output_to_operand_aliasing={{}: (3, {})} | custom-call | tf_op jit(solution)/shard_map/feedback/pallas_call | solution.py:363
  111.3 1.5 %collective-permute-start.23 = (f32[8,256]{1,0:T(8,128)S(1)}, f32[8,256]{1,0:T(8,128)S(1)}, u32[]{:S(2)}, u32[]{:S(2)}) collective-permute-start(f32[8,256]{1,0:T(8,128)S(1)} %get-tuple-element.55.norm_ref), channel_id=1, source_target_pairs={{0,1},{1,0},{2,3},{3,2},{4,5},{5,4},{6,7},{7,6},{8,9},{9,8},{10,11... | collective-permute-start | bytes 24584 | tf_op jit(solution)/shard_map/ppermute | solution.py:520
  112.8 4.0 %fetch_weights.1.w_ref = f32[2048,1024]{1,0:T(8,128)S(1)} custom-call(s32[3]{0:T(128)S(1)} %pad_add_fusion.at_ref, f32[2,2048,1024]{2,1,0:T(8,128)} %w_ref.3, bf16[256,256]{1,0:T(8,128)(2,1)S(1)} %get-tuple-element.63.refs_0_.after_ref), custom_call_target="tpu_custom_call" | custom-call | tf_op jit(solution)/shard_map/fetch_weights/pallas_call | solution.py:199
  116.9 6.6 %update_own.1 = (f32[2,2048,1024]{2,1,0:T(8,128)}, f32[128,1024]{1,0:T(8,128)S(1)}, f32[128,1024]{1,0:T(8,128)S(1)}) custom-call(s32[3]{0:T(128)S(1)} %pad_add_fusion.at_ref, f32[2048,1024]{1,0:T(8,128)S(1)} %fetch_weights.1.w_ref, bf16[2048,256]{1,0:T(8,128)(2,1)S(1)} %get-tuple-element.32.raw_ref, f32[8,256]{1,0:T(8,128)S(1)} %get-tuple-element.46.scale_ref, ...), custom_call_target="tpu_custom_call" | custom-call | tf_op jit(solution)/shard_map/update_own/pallas_call | solution.py:436
  123.7 0.4 collective-permute-start.24
  124.1 1.6 %collective-permute-done.24.rest_1_ = f32[128,256]{1,0:T(8,128)S(1)} collective-permute-done((f32[128,256]{1,0:T(8,128)S(1)}, f32[128,256]{1,0:T(8,128)S(1)}, u32[]{:S(2)}, u32[]{:S(2)}) %collective-permute-start.24) | collective-permute-done | bytes 131104 | tf_op jit(solution)/shard_map/ppermute | solution.py:43
  125.7 8.3 %update_other.1 = (f32[2,2048,1024]{2,1,0:T(8,128)}, f32[128,1024]{1,0:T(8,128)S(1)}, f32[128,1024]{1,0:T(8,128)S(1)}) custom-call(s32[3]{0:T(128)S(1)} %pad_add_fusion.at_ref, f32[2,2048,1024]{2,1,0:T(8,128)} %w_ref.3, bf16[2048,256]{1,0:T(8,128)(2,1)S(1)} %collective-permute-done.22.raw_ref, ...), custom_call_target="tpu_custom_call", output_to_operand_aliasing={{0}: (9, {})} | custom-call | tf_op jit(solution)/shard_map/update_other/pallas_call | solution.py:436
  134.2 2.0 %factor_share.1 = f32[2048,128]{1,0:T(8,128)} custom-call(s32[3]{0:T(128)S(1)} %pad_add_fusion.at_ref, f32[256,2048]{1,0:T(8,128)S(1)} %get-tuple-element.43.right_ref, f32[8,256]{1,0:T(8,128)S(1)} %get-tuple-element.55.norm_ref), custom_call_target="tpu_custom_call" | custom-call | tf_op jit(solution)/shard_map/factor_share/pallas_call | solution.py:329
  136.3 1.5 %finish.1 = bf16[128,1024]{1,0:T(8,128)(2,1)} custom-call(s32[3]{0:T(128)S(1)} %pad_add_fusion.at_ref, f32[128,1024]{1,0:T(8,128)S(1)} %get-tuple-element.50.refs_0_, f32[128,1024]{1,0:T(8,128)S(1)} %collective-permute-done.26.refs_1_, f32[128,1024]{1,0:T(8,128)S(1)} %get-tuple-element.52.refs_2_, f32[128,1024]{1,0:T(8,128)S(1)} %collective-permute-done.27.refs_3_), custom_call_target="tpu_custom_call" | custom-call | tf_op jit(solution)/shard_map/finish/pallas_call | solution.py:471
  (35 shorter events, 1.2 us)
Async XLA Ops:
  1.9 2.1 %collective-permute-start = (bf16[2048,128]{1,0:T(8,128)(2,1)S(1)}, bf16[2048,128]{1,0:T(8,128)(2,1)S(1)}, u32[]{:S(2)}, u32[]{:S(2)}) collective-permute-start(bf16[2048,128]{1,0:T(8,128)(2,1)S(1)} %convert_bitcast_fusion), channel_id=1, source_target_pairs={{0,16},{16,0},{1,17},{17,1},{2,18},{18,2},{3,19},{19,3},{4,20},{20... | collective-permute-start | bytes 1572872 | tf_op jit(solution)/shard_map/ppermute | solution.py:30
  15.1 8.8 %collective-permute-start.1 = (bf16[256,256]{1,0:T(8,128)(2,1)S(1)}, bf16[256,256]{1,0:T(8,128)(2,1)S(1)}, u32[]{:S(2)}, u32[]{:S(2)}) collective-permute-start(bf16[256,256]{1,0:T(8,128)(2,1)S(1)} %get-tuple-element.62), channel_id=1, source_target_pairs={{0,2},{2,0},{4,6},{6,4},{8,10},{10,8},{12,14},{14,12},{1,3},{3,1},... | collective-permute-start | bytes 393224 | tf_op jit(solution)/shard_map/ppermute | solution.py:43
  18.0 10.8 %collective-permute-start.2 = (bf16[256,256]{1,0:T(8,128)(2,1)S(1)}, bf16[256,256]{1,0:T(8,128)(2,1)S(1)}, u32[]{:S(2)}, u32[]{:S(2)}) collective-permute-start(bf16[256,256]{1,0:T(8,128)(2,1)S(1)} %get-tuple-element.61), channel_id=1, source_target_pairs={{0,4},{2,6},{4,0},{6,2},{8,12},{10,14},{12,8},{14,10},{1,5},{3,7},... | collective-permute-start | bytes 393224 | tf_op jit(solution)/shard_map/ppermute | solution.py:43
  19.6 10.5 %collective-permute-start.3 = (bf16[256,256]{1,0:T(8,128)(2,1)S(1)}, bf16[256,256]{1,0:T(8,128)(2,1)S(1)}, u32[]{:S(2)}, u32[]{:S(2)}) collective-permute-start(bf16[256,256]{1,0:T(8,128)(2,1)S(1)} %get-tuple-element.60), channel_id=1, source_target_pairs={{0,6},{2,4},{4,2},{6,0},{8,14},{10,12},{12,10},{14,8},{1,7},{3,5},... | collective-permute-start | bytes 393224 | tf_op jit(solution)/shard_map/ppermute | solution.py:43
  19.6 10.5 %collective-permute-start.4 = (bf16[256,256]{1,0:T(8,128)(2,1)S(1)}, bf16[256,256]{1,0:T(8,128)(2,1)S(1)}, u32[]{:S(2)}, u32[]{:S(2)}) collective-permute-start(bf16[256,256]{1,0:T(8,128)(2,1)S(1)} %get-tuple-element.59), channel_id=1, source_target_pairs={{0,8},{2,10},{4,12},{6,14},{8,0},{10,2},{12,4},{14,6},{1,9},{3,11}... | collective-permute-start | bytes 393224 | tf_op jit(solution)/shard_map/ppermute | solution.py:43
  22.6 19.1 %collective-permute-start.5 = (bf16[256,256]{1,0:T(8,128)(2,1)S(1)}, bf16[256,256]{1,0:T(8,128)(2,1)S(1)}, u32[]{:S(2)}, u32[]{:S(2)}) collective-permute-start(bf16[256,256]{1,0:T(8,128)(2,1)S(1)} %get-tuple-element.58), channel_id=1, source_target_pairs={{0,10},{2,8},{4,14},{6,12},{8,2},{10,0},{12,6},{14,4},{1,11},{3,9}... | collective-permute-start | bytes 393224 | tf_op jit(solution)/shard_map/ppermute | solution.py:43
  23.9 17.8 %collective-permute-start.6 = (bf16[256,256]{1,0:T(8,128)(2,1)S(1)}, bf16[256,256]{1,0:T(8,128)(2,1)S(1)}, u32[]{:S(2)}, u32[]{:S(2)}) collective-permute-start(bf16[256,256]{1,0:T(8,128)(2,1)S(1)} %get-tuple-element.57), channel_id=1, source_target_pairs={{0,12},{2,14},{4,8},{6,10},{8,4},{10,6},{12,0},{14,2},{1,13},{3,15... | collective-permute-start | bytes 393224 | tf_op jit(solution)/shard_map/ppermute | solution.py:43
  28.8 12.9 %collective-permute-start.7 = (bf16[256,256]{1,0:T(8,128)(2,1)S(1)}, bf16[256,256]{1,0:T(8,128)(2,1)S(1)}, u32[]{:S(2)}, u32[]{:S(2)}) collective-permute-start(bf16[256,256]{1,0:T(8,128)(2,1)S(1)} %get-tuple-element.56), channel_id=1, source_target_pairs={{0,14},{2,12},{4,10},{6,8},{8,6},{10,4},{12,2},{14,0},{1,15},{3,13... | collective-permute-start | bytes 393224 | tf_op jit(solution)/shard_map/ppermute | solution.py:43
  41.8 13.2 %collective-permute-start.10 = (bf16[256,256]{1,0:T(8,128)(2,1)S(1)}, bf16[256,256]{1,0:T(8,128)(2,1)S(1)}, u32[]{:S(2)}, u32[]{:S(2)}) collective-permute-start(bf16[256,256]{1,0:T(8,128)(2,1)S(1)} %block_sum.1.refs_0_), channel_id=1, source_target_pairs={{0,6},{2,4},{4,2},{6,0},{8,14},{10,12},{12,10},{14,8},{1,7},{3,5},... | collective-permute-start | bytes 393224 | tf_op jit(solution)/shard_map/ppermute | solution.py:43
  47.4 17.5 %collective-permute-start.11 = (bf16[256,256]{1,0:T(8,128)(2,1)S(1)}, bf16[256,256]{1,0:T(8,128)(2,1)S(1)}, u32[]{:S(2)}, u32[]{:S(2)}) collective-permute-start(bf16[256,256]{1,0:T(8,128)(2,1)S(1)} %block_sum.1.refs_0_), channel_id=1, source_target_pairs={{0,8},{2,10},{4,12},{6,14},{8,0},{10,2},{12,4},{14,6},{1,9},{3,11}... | collective-permute-start | bytes 393224 | tf_op jit(solution)/shard_map/ppermute | solution.py:43
  49.2 20.0 %collective-permute-start.12 = (bf16[256,256]{1,0:T(8,128)(2,1)S(1)}, bf16[256,256]{1,0:T(8,128)(2,1)S(1)}, u32[]{:S(2)}, u32[]{:S(2)}) collective-permute-start(bf16[256,256]{1,0:T(8,128)(2,1)S(1)} %block_sum.1.refs_0_), channel_id=1, source_target_pairs={{0,10},{2,8},{4,14},{6,12},{8,2},{10,0},{12,6},{14,4},{1,11},{3,9}... | collective-permute-start | bytes 393224 | tf_op jit(solution)/shard_map/ppermute | solution.py:43
  51.1 18.2 %collective-permute-start.13 = (bf16[256,256]{1,0:T(8,128)(2,1)S(1)}, bf16[256,256]{1,0:T(8,128)(2,1)S(1)}, u32[]{:S(2)}, u32[]{:S(2)}) collective-permute-start(bf16[256,256]{1,0:T(8,128)(2,1)S(1)} %block_sum.1.refs_0_), channel_id=1, source_target_pairs={{0,12},{2,14},{4,8},{6,10},{8,4},{10,6},{12,0},{14,2},{1,13},{3,15... | collective-permute-start | bytes 393224 | tf_op jit(solution)/shard_map/ppermute | solution.py:43
  54.4 14.8 %collective-permute-start.14 = (bf16[256,256]{1,0:T(8,128)(2,1)S(1)}, bf16[256,256]{1,0:T(8,128)(2,1)S(1)}, u32[]{:S(2)}, u32[]{:S(2)}) collective-permute-start(bf16[256,256]{1,0:T(8,128)(2,1)S(1)} %block_sum.1.refs_0_), channel_id=1, source_target_pairs={{0,14},{2,12},{4,10},{6,8},{8,6},{10,4},{12,2},{14,0},{1,15},{3,13... | collective-permute-start | bytes 393224 | tf_op jit(solution)/shard_map/ppermute | solution.py:43
  55.0 14.2 %collective-permute-start.8 = (bf16[256,256]{1,0:T(8,128)(2,1)S(1)}, bf16[256,256]{1,0:T(8,128)(2,1)S(1)}, u32[]{:S(2)}, u32[]{:S(2)}) collective-permute-start(bf16[256,256]{1,0:T(8,128)(2,1)S(1)} %block_sum.1.refs_0_), channel_id=1, source_target_pairs={{0,2},{2,0},{4,6},{6,4},{8,10},{10,8},{12,14},{14,12},{1,3},{3,1},... | collective-permute-start | bytes 393224 | tf_op jit(solution)/shard_map/ppermute | solution.py:43
  64.9 5.0 %collective-permute-start.9 = (bf16[256,256]{1,0:T(8,128)(2,1)S(1)}, bf16[256,256]{1,0:T(8,128)(2,1)S(1)}, u32[]{:S(2)}, u32[]{:S(2)}) collective-permute-start(bf16[256,256]{1,0:T(8,128)(2,1)S(1)} %block_sum.1.refs_0_), channel_id=1, source_target_pairs={{0,4},{2,6},{4,0},{6,2},{8,12},{10,14},{12,8},{14,10},{1,5},{3,7},... | collective-permute-start | bytes 393224 | tf_op jit(solution)/shard_map/ppermute | solution.py:43
  73.5 11.4 %collective-permute-start.17 = (bf16[256,2048]{1,0:T(8,128)(2,1)S(1)}, bf16[256,2048]{1,0:T(8,128)(2,1)S(1)}, u32[]{:S(2)}, u32[]{:S(2)}) collective-permute-start(bf16[256,2048]{1,0:T(8,128)(2,1)S(1)} %get-tuple-element.36), channel_id=1, source_target_pairs={{0,16},{16,0},{1,17},{17,1},{2,18},{18,2},{3,19},{19,3},{4,20},{20... | collective-permute-start | bytes 3145736 | tf_op jit(solution)/shard_map/ppermute | solution.py:504
  73.6 50.5 %collective-permute-start.22 = (bf16[2048,256]{1,0:T(8,128)(2,1)S(1)}, bf16[2048,256]{1,0:T(8,128)(2,1)S(1)}, u32[]{:S(2)}, u32[]{:S(2)}) collective-permute-start(bf16[2048,256]{1,0:T(8,128)(2,1)S(1)} %get-tuple-element.32.raw_ref), channel_id=1, source_target_pairs={{0,1},{1,0},{2,3},{3,2},{4,5},{5,4},{6,7},{7,6},{8,9},{9,8},{10,11... | collective-permute-start | bytes 3145736 | tf_op jit(solution)/shard_map/ppermute | solution.py:498
  75.2 1.5 %collective-permute-start.15 = (f32[256,256]{1,0:T(8,128)S(1)}, f32[256,256]{1,0:T(8,128)S(1)}, u32[]{:S(2)}, u32[]{:S(2)}) collective-permute-start(f32[256,256]{1,0:T(8,128)S(1)} %get-tuple-element.30), channel_id=1, source_target_pairs={{0,16},{16,0},{1,17},{17,1},{2,18},{18,2},{3,19},{19,3},{4,20},{20... | collective-permute-start | bytes 786440 | tf_op jit(solution)/shard_map/ppermute | solution.py:38
  87.3 24.0 %collective-permute-start.18 = (bf16[128,1024]{1,0:T(8,128)(2,1)S(1)}, bf16[128,1024]{1,0:T(8,128)(2,1)S(1)}, u32[]{:S(2)}, u32[]{:S(2)}) collective-permute-start(bf16[128,1024]{1,0:T(8,128)(2,1)S(1)} %get-tuple-element.37), channel_id=1, source_target_pairs={{0,1},{1,0},{2,3},{3,2},{4,5},{5,4},{6,7},{7,6},{8,9},{9,8},{10,11... | collective-permute-start | bytes 786440 | tf_op jit(solution)/shard_map/ppermute | solution.py:510
  88.7 3.7 %collective-permute-start.19 = (f32[8,256]{1,0:T(8,128)S(1)}, f32[8,256]{1,0:T(8,128)S(1)}, u32[]{:S(2)}, u32[]{:S(2)}) collective-permute-start(f32[8,256]{1,0:T(8,128)S(1)} %get-tuple-element.38), channel_id=1, source_target_pairs={{0,2},{2,0},{4,6},{6,4},{8,10},{10,8},{12,14},{14,12},{1,3},{3,1},... | collective-permute-start | bytes 24584 | tf_op jit(solution)/shard_map/ppermute | solution.py:517
  92.5 5.5 %collective-permute-start.20 = (f32[8,256]{1,0:T(8,128)S(1)}, f32[8,256]{1,0:T(8,128)S(1)}, u32[]{:S(2)}, u32[]{:S(2)}) collective-permute-start(f32[8,256]{1,0:T(8,128)S(1)} %add.19), channel_id=1, source_target_pairs={{0,4},{2,6},{4,0},{6,2},{8,12},{10,14},{12,8},{14,10},{1,5},{3,7},... | collective-permute-start | bytes 24584 | tf_op jit(solution)/shard_map/ppermute | solution.py:517
  97.9 13.3 %collective-permute-start.21 = (f32[8,256]{1,0:T(8,128)S(1)}, f32[8,256]{1,0:T(8,128)S(1)}, u32[]{:S(2)}, u32[]{:S(2)}) collective-permute-start(f32[8,256]{1,0:T(8,128)S(1)} %add.20), channel_id=1, source_target_pairs={{0,8},{2,10},{4,12},{6,14},{8,0},{10,2},{12,4},{14,6},{1,9},{3,11}... | collective-permute-start | bytes 24584 | tf_op jit(solution)/shard_map/ppermute | solution.py:517
  101.0 10.2 %collective-permute-start.16 = (f32[128,256]{1,0:T(8,128)S(1)}, f32[128,256]{1,0:T(8,128)S(1)}, u32[]{:S(2)}, u32[]{:S(2)}) collective-permute-start(f32[128,256]{1,0:T(8,128)S(1)} %get-tuple-element.31), channel_id=1, source_target_pairs={{0,1},{1,0},{2,3},{3,2},{4,5},{5,4},{6,7},{7,6},{8,9},{9,8},{10,11... | collective-permute-start | bytes 393224 | tf_op jit(solution)/shard_map/ppermute | solution.py:506
  111.2 5.7 %copy-start = (bf16[256,2048]{1,0:T(8,128)(2,1)S(1)}, bf16[256,2048]{1,0:T(8,128)(2,1)}, u32[]{:S(2)}) copy-start(bf16[256,2048]{1,0:T(8,128)(2,1)} %tok_ref.3) | copy-start | bytes 3145732
  111.3 14.4 %collective-permute-start.25 = (bf16[128,1024]{1,0:T(8,128)(2,1)S(1)}, bf16[128,1024]{1,0:T(8,128)(2,1)S(1)}, u32[]{:S(2)}, u32[]{:S(2)}) collective-permute-start(bf16[128,1024]{1,0:T(8,128)(2,1)S(1)} %collective-permute-done.18.rest_2_), channel_id=1, source_target_pairs={{0,16},{16,0},{1,17},{17,1},{2,18},{18,2},{3,19},{19,3},{4,20},{20... | collective-permute-start | bytes 786440 | tf_op jit(solution)/shard_map/ppermute | solution.py:43
  111.3 12.8 %collective-permute-start.23 = (f32[8,256]{1,0:T(8,128)S(1)}, f32[8,256]{1,0:T(8,128)S(1)}, u32[]{:S(2)}, u32[]{:S(2)}) collective-permute-start(f32[8,256]{1,0:T(8,128)S(1)} %get-tuple-element.55.norm_ref), channel_id=1, source_target_pairs={{0,1},{1,0},{2,3},{3,2},{4,5},{5,4},{6,7},{7,6},{8,9},{9,8},{10,11... | collective-permute-start | bytes 24584 | tf_op jit(solution)/shard_map/ppermute | solution.py:520
  123.5 12.7 %collective-permute-start.26 = (f32[128,1024]{1,0:T(8,128)S(1)}, f32[128,1024]{1,0:T(8,128)S(1)}, u32[]{:S(2)}, u32[]{:S(2)}) collective-permute-start(f32[128,1024]{1,0:T(8,128)S(1)} %get-tuple-element.51), channel_id=1, source_target_pairs={{0,16},{16,0},{1,17},{17,1},{2,18},{18,2},{3,19},{19,3},{4,20},{20... | collective-permute-start | bytes 1572872 | tf_op jit(solution)/shard_map/ppermute | solution.py:43
  123.7 1.9 %collective-permute-start.24 = (f32[128,256]{1,0:T(8,128)S(1)}, f32[128,256]{1,0:T(8,128)S(1)}, u32[]{:S(2)}, u32[]{:S(2)}) collective-permute-start(f32[128,256]{1,0:T(8,128)S(1)} %collective-permute-done.16.rest_0_), channel_id=1, source_target_pairs={{0,16},{16,0},{1,17},{17,1},{2,18},{18,2},{3,19},{19,3},{4,20},{20... | collective-permute-start | bytes 393224 | tf_op jit(solution)/shard_map/ppermute | solution.py:43
  134.0 2.3 %collective-permute-start.27 = (f32[128,1024]{1,0:T(8,128)S(1)}, f32[128,1024]{1,0:T(8,128)S(1)}, u32[]{:S(2)}, u32[]{:S(2)}) collective-permute-start(f32[128,1024]{1,0:T(8,128)S(1)} %get-tuple-element.53), channel_id=1, source_target_pairs={{0,16},{16,0},{1,17},{17,1},{2,18},{18,2},{3,19},{19,3},{4,20},{20... | collective-permute-start | bytes 1572872 | tf_op jit(solution)/shard_map/ppermute | solution.py:43

commit v2 on v1

--- a/solution.py
+++ b/solution.py
@@ -41,6 +41,25 @@
 
 def send_all(blocks, axis, n):
     return [lax.ppermute(blocks[k], axis, peers(n, k)) for k in range(1, n)]
+
+
+class Grid:
+    def __init__(self, n, size):
+        self.n, self.size = n, size
+        self.nx = max(x for x in bits_of(n) + [n] if x * x <= n)
+        self.nz = n // self.nx
+        self.head = size if size < 48 else (size * 2 // 3 + 15) // 16 * 16
+        self.tail = size - self.head
+
+    def send_x(self, blocks):
+        return [lax.ppermute(b, "col", peers(self.n, k)) for k, b in enumerate(blocks, 1)]
+
+    def send_z(self, blocks):
+        return [lax.ppermute(b, "col", peers(self.n, k * self.nx)) for k, b in enumerate(blocks, 1)]
+
+
+def ds(i, n):
+    return slice(i * n, (i + 1) * n)
 
 
 def stacked(x, order):
@@ -133,7 +152,9 @@
     return min(256, width)
 
 
-def load_kernel(at_ref, m_ref, g_ref, q_ref, buf_ref, left_ref, grad_ref, sem_m, sem_g):
+def load_kernel(at_ref, m_ref, g_ref, q_ref, buf_ref, *rest, grid):
+    outs = rest[:-4]
+    left_ref, grad_ref, sem_m, sem_g = rest[-4:]
     width = buf_ref.shape[0]
     _, size, _ = left_ref.shape
     ch = rows_per_step(width)
@@ -156,37 +177,52 @@
         part = dot(buf.astype(bf16), q_ref[...]).astype(bf16)
         for r in range(0, ch, size):
             left_ref[at_ref[1] ^ ((i * ch + r) // size)] = part[r : r + size, :]
-
-
-def load_left(place, m, g, q, blocks):
+    for x in range(grid.nx):
+        for z in range(grid.nz):
+            outs[x][ds(z, grid.head), :] = left_ref[x + grid.nx * z, : grid.head, :]
+    if grid.tail:
+        for z in range(grid.nz):
+            for x in range(grid.nx):
+                outs[grid.nx + z][ds(x, grid.tail), :] = left_ref[x + grid.nx * z, grid.head :, :]
+
+
+def load_left(place, m, g, q, grid):
     width, hid = m.shape
+    rank = q.shape[1]
+    blocks = grid.n
     n = width // rows_per_step(width)
     assert rows_per_step(width) % (width // blocks) == 0
-    return pl.pallas_call(
-        load_kernel,
-        out_shape=(
-            pltpu.VMEM((width, hid), f32),
-            pltpu.VMEM((blocks, width // blocks, q.shape[1]), bf16),
-        ),
+    outs = [pltpu.VMEM((grid.nz * grid.head, rank), bf16)] * grid.nx
+    if grid.tail:
+        outs += [pltpu.VMEM((grid.nx * grid.tail, rank), bf16)] * grid.nz
+    buf, *outs = pl.pallas_call(
+        functools.partial(load_kernel, grid=grid),
+        out_shape=(pltpu.VMEM((width, hid), f32), *outs),
         in_specs=[SM, HB, HB, VM],
-        out_specs=(VM, VM),
-        scratch_shapes=[pltpu.VMEM((width, hid), bf16), DMA((n,)), DMA((n,))],
+        out_specs=(VM,) * (1 + len(outs)),
+        scratch_shapes=[
+            pltpu.VMEM((blocks, width // blocks, rank), bf16),
+            pltpu.VMEM((width, hid), bf16),
+            DMA((n,)),
+            DMA((n,)),
+        ],
         compiler_params=params(16),
         name="load_left",
     )(place, in_hbm(m), in_hbm(g), q)
+    return buf, outs[: grid.nx], outs[grid.nx :]
 
 
 def in_hbm(x):
     return pltpu.with_memory_space_constraint(x, pltpu.HBM)
 
 
-def fetch_kernel(at_ref, w_ref, after_ref, out_ref, sem):
+def fetch_kernel(at_ref, w_ref, after_ref, out_ref, sem, *, other):
     copies = []
     ch = rows_per_step(w_ref.shape[1])
     for i in range(w_ref.shape[1] // ch):
         at = pl.ds(i * ch, ch)
         copies.append(
-            pltpu.make_async_copy(w_ref.at[at_ref[2], at], out_ref.at[at], sem.at[i])
+            pltpu.make_async_copy(w_ref.at[at_ref[2] ^ other, at], out_ref.at[at], sem.at[i])
         )
     for c in copies:
         c.start()
@@ -194,10 +230,10 @@
         c.wait()
 
 
-def fetch(place, w, after):
+def fetch(place, w, after, other):
     n = w.shape[1] // rows_per_step(w.shape[1])
     return pl.pallas_call(
-        fetch_kernel,
+        functools.partial(fetch_kernel, other=other),
         out_shape=pltpu.VMEM(w.shape[1:], w.dtype),
         in_specs=[SM, HB, VM],
         out_specs=VM,
@@ -207,46 +243,137 @@
     )(place, w, after)
 
 
-def sum_kernel(*refs):
-    total = refs[0][...].astype(f32)
-    for r in refs[1:-1]:
-        total = total + r[...].astype(f32)
-    refs[-1][...] = total.astype(bf16)
-
-
-def block_sum(blocks):
-    return pl.pallas_call(
-        sum_kernel,
-        out_shape=pltpu.VMEM(blocks[0].shape, bf16),
-        in_specs=[VM] * len(blocks),
-        out_specs=VM,
+def add_up(refs, rows):
+    total = refs[0][rows, :].astype(f32)
+    for r in refs[1:]:
+        total = total + r[rows, :].astype(f32)
+    return total.astype(bf16)
+
+
+def halfway_kernel(*refs, grid):
+    heads, tails = refs[: grid.nx], refs[grid.nx : grid.nx + (grid.nz if grid.tail else 0)]
+    outs = refs[len(heads) + len(tails) :]
+    for z in range(grid.nz):
+        outs[z][...] = add_up(heads, ds(z, grid.head))
+    if grid.tail:
+        for x in range(grid.nx):
+            outs[grid.nz + x][...] = add_up(tails, ds(x, grid.tail))
+
+
+def halfway(grid, heads, tails):
+    rank = heads[0].shape[1]
+    outs = [pltpu.VMEM((grid.head, rank), bf16)] * grid.nz
+    if grid.tail:
+        outs += [pltpu.VMEM((grid.tail, rank), bf16)] * grid.nx
+    outs = pl.pallas_call(
+        functools.partial(halfway_kernel, grid=grid),
+        out_shape=tuple(outs),
+        in_specs=[VM] * (len(heads) + len(tails)),
+        out_specs=(VM,) * len(outs),
+        compiler_params=params(4),
+        name="halfway",
+    )(*heads, *tails)
+    return list(outs[: grid.nz]), list(outs[grid.nz :])
+
+
+def block_kernel(*refs, grid):
+    n = grid.nz
+    refs[-2 if grid.tail else -1][...] = add_up(refs[:n], slice(None))
+    if grid.tail:
+        refs[-1][...] = add_up(refs[n : n + grid.nx], slice(None))
+
+
+def block_sum(grid, heads, tails):
+    rank = heads[0].shape[1]
+    outs = [pltpu.VMEM((grid.head, rank), bf16)]
+    if grid.tail:
+        outs += [pltpu.VMEM((grid.tail, rank), bf16)]
+    outs = pl.pallas_call(
+        functools.partial(block_kernel, grid=grid),
+        out_shape=tuple(outs),
+        in_specs=[VM] * (len(heads) + len(tails)),
+        out_specs=(VM,) * len(outs),
         compiler_params=params(4),
         name="block_sum",
-    )(*blocks)
-
-
-def gram_kernel(at_ref, *refs):
-    blocks, raw_ref, gram_ref = refs[:-2], refs[-2], refs[-1]
-    size = blocks[0].shape[0]
-    for k, r in enumerate(blocks):
-        start = pl.multiple_of((at_ref[1] ^ k) * size, size)
-        raw_ref[pl.ds(start, size), :] = r[...]
+    )(*heads, *tails)
+    return outs[0], (outs[1] if grid.tail else None)
+
+
+def stack_kernel(*refs, sizes):
+    outs = refs[-len(sizes) :]
+    at = 0
+    for out, n in zip(outs, sizes):
+        for k in range(n):
+            out[ds(k, refs[at].shape[0]), :] = refs[at][...]
+            at += 1
+
+
+def stack_rows(*groups):
+    groups = [g for g in groups if g]
+    flat = [b for g in groups for b in g]
+    outs = tuple(
+        pltpu.VMEM((len(g) * g[0].shape[0], g[0].shape[1]), g[0].dtype) for g in groups
+    )
+    return pl.pallas_call(
+        functools.partial(stack_kernel, sizes=tuple(len(g) for g in groups)),
+        out_shape=outs,
+        in_specs=[VM] * len(flat),
+        out_specs=(VM,) * len(outs),
+        compiler_params=params(4),
+        name="stack_rows",
+    )(*flat)
+
+
+def gram_kernel(at_ref, *refs, grid):
+    heads, tails, (raw_ref, rest_ref, gram_ref) = refs[: grid.nx], refs[grid.nx : -3], refs[-3:]
+    spread_rows(at_ref, grid, heads, tails, raw_ref)
+    at = 0
+    for r in heads[1:] + tails[1:]:
+        rest_ref[at : at + r.shape[0], :] = r[...]
+        at += r.shape[0]
     raw = raw_ref[...]
     gram_ref[...] = lax.dot_general(
         raw, raw, (((0,), (0,)), ((), ())), preferred_element_type=f32
     )
 
 
-def join_gram(place, blocks):
-    size, rank = blocks[0].shape
-    return pl.pallas_call(
-        gram_kernel,
-        out_shape=(pltpu.VMEM((size * len(blocks), rank), bf16), pltpu.VMEM((rank, rank), f32)),
-        in_specs=[SM] + [VM] * len(blocks),
-        out_specs=(VM, VM),
+def join_gram(place, grid, heads, tails):
+    rank = heads[0].shape[1]
+    rest = sum(r.shape[0] for r in heads[1:] + tails[1:])
+    return pl.pallas_call(
+        functools.partial(gram_kernel, grid=grid),
+        out_shape=(
+            pltpu.VMEM((grid.size * grid.n, rank), bf16),
+            pltpu.VMEM((rest, rank), bf16),
+            pltpu.VMEM((rank, rank), f32),
+        ),
+        in_specs=[SM] + [VM] * (len(heads) + len(tails)),
+        out_specs=(VM, VM, VM),
         compiler_params=params(6),
         name="join_gram",
-    )(place, *blocks)
+    )(place, *heads, *tails)
+
+
+def sum_scatter_gather(place, grid, heads, tails, swap, cover):
+    got_z = grid.send_z(tails[1:])
+    got_x = grid.send_x(heads[1:])
+    own = cover(heads[0], 0)
+    heads, tails = halfway(grid, heads[:1] + got_x, tails[:1] + got_z)
+    got_z = grid.send_z(heads[1:])
+    got_x = grid.send_x(tails[1:])
+    head, tail = block_sum(grid, heads[:1] + got_z, tails[:1] + got_x)
+    heads = [head] + grid.send_z([head] * (grid.nz - 1))
+    tails = [tail] + grid.send_x([tail] * (grid.nx - 1)) if grid.tail else []
+    other = cover(head, 1)
+    stacks = stack_rows(heads, tails)
+    raws = [lax.ppermute(x, "grp", swap) for x in stacks]
+    tails = grid.send_z([stacks[1]] * (grid.nz - 1)) if grid.tail else []
+    heads = [stacks[0]] + grid.send_x([stacks[0]] * (grid.nx - 1))
+    if grid.tail:
+        tails = [stacks[1]] + tails
+    raw, rest, gram = join_gram(place, grid, heads, tails)
+    raws.append(lax.ppermute(rest, "grp", swap))
+    return raw, gram, raws, own, other
 
 
 def right_kernel(raw_ref, buf_ref, out_ref, outh_ref):
@@ -273,11 +400,13 @@
 
 
 def factors_kernel(
-    at_ref, raw_ref, inv_ref, rr_ref, rro_ref, left_ref, right_ref, righth_ref, own_ref, part_ref, sq_ref,
+    at_ref, raw_ref, inv_ref, rr_ref, rro_ref, leftf_ref, left_ref, right_ref, righth_ref, own_ref, part_ref, sq_ref,
     split_ref,
 ):
     inv_hi, inv_lo = split(inv_ref[...])
-    left_ref[...] = (dot_t(raw_ref[...], inv_hi) + dot_t(raw_ref[...], inv_lo)).astype(bf16)
+    left = dot_t(raw_ref[...], inv_hi) + dot_t(raw_ref[...], inv_lo)
+    leftf_ref[...] = left
+    left_ref[...] = left.astype(bf16)
     hid = rr_ref.shape[1]
     half = split_ref.shape[2]
     ch = min(512, half)
@@ -302,6 +431,7 @@
     return pl.pallas_call(
         factors_kernel,
         out_shape=(
+            pltpu.VMEM(raw.shape, f32),
             pltpu.VMEM(raw.shape, bf16),
             pltpu.VMEM((rank, hid), f32),
             pltpu.VMEM((rank, hid), bf16),
@@ -310,7 +440,7 @@
             pltpu.VMEM((8, rank), f32),
         ),
         in_specs=[SM, VM, VM, VM, VM],
-        out_specs=(VM, VM, VM, VM, VM, VM),
+        out_specs=(VM,) * 7,
         scratch_shapes=[pltpu.VMEM((groups, rank, hid // groups), bf16)],
         compiler_params=params(6),
         name="factors",
@@ -372,86 +502,148 @@
     )(*args)
 
 
-WSLOTS = 4
-
-
-def update_kernel(at_ref, w_ref, raw_ref, scale_ref, tok_ref, *rest, other, shares):
-    n = shares if other else 1
-    if other:
-        rest, near_ref, wsem = rest[:-2], rest[-2], rest[-1]
-    invs, rights = rest[:n], rest[n : 2 * n]
-    out_ref, decs = rest[-6 - shares], rest[-5 - shares : -5]
-    inv_ref, right_ref, stage_ref, acc_ref, sem = rest[-5:]
-    width = raw_ref.shape[0]
-    ch = rows_per_step(width)
-    p = at_ref[2] ^ other
-    reads = []
-    if other:
-        for i, r in enumerate(range(0, width, ch)):
-            at = pl.ds(r, ch)
-            reads.append(pltpu.make_async_copy(w_ref.at[p, at], near_ref.at[at], wsem.at[i]))
-            reads[-1].start()
-        w_ref = near_ref
-    for j in range(n):
-        rows = invs[j].shape[0]
-        at = pl.ds(pl.multiple_of((at_ref[0] ^ j) * rows, rows), rows) if other else slice(None)
-        inv_ref[at, :] = invs[j][...]
-        right_ref[at, :] = rights[j][...]
+WSLOTS = 3
+
+
+def spread_rows(at_ref, grid, heads, tails, out_ref):
+    for x in range(grid.nx):
+        for z in range(grid.nz):
+            start = (at_ref[1] ^ (x + grid.nx * z)) * grid.size
+            at = pl.ds(pl.multiple_of(start, 16), grid.head)
+            out_ref[at, :] = heads[x][ds(z, grid.head), :]
+            if grid.tail:
+                at = pl.ds(pl.multiple_of(start + grid.head, 16), grid.tail)
+                out_ref[at, :] = tails[z][ds(x, grid.tail), :]
+
+
+def update_rows(p, w_ref, left_of, right, tok_ref, out_ref, stage_ref, sem):
+    width = w_ref.shape[0]
+    ch = stage_ref.shape[1]
     pending = []
-    share = decs[0].shape[0]
-    hi, lo = split(inv_ref[...])
-    scale = scale_ref[0:1, :]
-    right = right_ref[...]
     acc = None
     for r in range(0, width, ch):
         at = pl.ds(r, ch)
         slot = len(pending) % WSLOTS
         if len(pending) >= WSLOTS:
             pending[len(pending) - WSLOTS].wait()
-        raw = raw_ref[at, :]
-        left = ((dot_t(raw, hi) + dot_t(raw, lo)) * scale).astype(bf16)
-        if other:
-            reads[r // ch].wait()
-        new = w_ref[at, :] - dot(left, right)
+        new = w_ref[at, :] - dot(left_of(at), right)
         stage_ref[slot] = new
         copy = pltpu.make_async_copy(stage_ref.at[slot], out_ref.at[p, at], sem.at[slot])
         copy.start()
         pending.append(copy)
         part = dot(tok_ref[:, at], new.astype(bf16))
         acc = part if acc is None else acc + part
+    return acc, pending[-WSLOTS:]
+
+
+def split_decode(at_ref, acc, acc_ref, decs):
+    share = decs[0].shape[0]
     acc_ref[...] = acc
     for j, dec in enumerate(decs):
         dec[...] = acc_ref[pl.ds(pl.multiple_of((at_ref[0] ^ j) * share, share), share), :]
-    for copy in pending[-WSLOTS:]:
+
+
+def own_kernel(at_ref, w_ref, left_ref, scale_ref, right_ref, tok_ref, out_ref, *rest):
+    decs, (stage_ref, acc_ref, sem) = rest[:-3], rest[-3:]
+    scale = scale_ref[0:1, :]
+    acc, pending = update_rows(
+        at_ref[2],
+        w_ref,
+        lambda at: (left_ref[at, :] * scale).astype(bf16),
+        right_ref[...],
+        tok_ref,
+        out_ref,
+        stage_ref,
+        sem,
+    )
+    split_decode(at_ref, acc, acc_ref, decs)
+    for copy in pending:
         copy.wait()
 
 
-def update(place, w, raw, scale, tokens, invs, rights, out, shares):
-    width, half = w.shape[-2:]
-    rank = raw.shape[1]
-    ch = rows_per_step(width)
-    other = out is not None
-    args = (place, w, raw, scale, tokens, *invs, *rights) + ((out,) if other else ())
+def other_kernel(at_ref, w_ref, scale_ref, tok_ref, *rest, grid, shares):
+    invs, rest = rest[:shares], rest[shares:]
+    rights, rest = rest[:shares], rest[shares:]
+    raws, out_ref, decs = rest[: -8 - shares], rest[-7 - shares], rest[-6 - shares : -6]
+    inv_ref, right_ref, raw_ref, stage_ref, acc_ref, sem = rest[-6:]
+    rows = invs[0].shape[0]
+    for j in range(shares):
+        at = pl.ds(pl.multiple_of((at_ref[0] ^ j) * rows, rows), rows)
+        inv_ref[at, :] = invs[j][...]
+        right_ref[at, :] = rights[j][...]
+    spread_parts(at_ref, grid, raws, raw_ref)
+    hi, lo = split(inv_ref[...])
+    scale = scale_ref[0:1, :]
+
+    def left_of(at):
+        raw = raw_ref[at, :]
+        return ((dot_t(raw, hi) + dot_t(raw, lo)) * scale).astype(bf16)
+
+    acc, pending = update_rows(
+        at_ref[2] ^ 1, w_ref, left_of, right_ref[...], tok_ref, out_ref, stage_ref, sem
+    )
+    split_decode(at_ref, acc, acc_ref, decs)
+    for copy in pending:
+        copy.wait()
+
+
+def spread_parts(at_ref, grid, raws, out_ref):
+    first, (rest_ref,) = raws[:-1], raws[-1:]
+    n, m = grid.nz * grid.head, grid.nx * grid.tail
+    heads = [first[0]] + [rest_ref.at[ds(k, n)] for k in range(grid.nx - 1)]
+    base = (grid.nx - 1) * n
+    tails = []
+    if grid.tail:
+        tails = [first[1]] + [
+            rest_ref.at[slice(base + k * m, base + (k + 1) * m)] for k in range(grid.nz - 1)
+        ]
+    spread_rows(at_ref, grid, heads, tails, out_ref)
+
+
+def update_shapes(w, tokens, shares):
+    width, half = w.shape
     batch = tokens.shape[0]
+    outs = (pltpu.HBM((2, width, half), f32),) + (pltpu.VMEM((batch // shares, half), f32),) * shares
+    scratch = [
+        pltpu.VMEM((WSLOTS, min(512, width), half), f32),
+        pltpu.VMEM((batch, half), f32),
+        DMA((WSLOTS,)),
+    ]
+    return outs, (HB,) + (VM,) * shares, scratch
+
+
+def update_own(place, w, left, scale, right, tokens, shares):
+    outs, specs, scratch = update_shapes(w, tokens, shares)
     new, *decs = pl.pallas_call(
-        functools.partial(update_kernel, other=int(other), shares=shares),
-        out_shape=(pltpu.HBM((2, width, half), f32),)
-        + (pltpu.VMEM((batch // shares, half), f32),) * shares,
-        in_specs=[SM, HB if other else VM]
-        + [VM] * (3 + len(invs) + len(rights))
-        + ([HB] if other else []),
-        out_specs=(HB,) + (VM,) * shares,
-        input_output_aliases={len(args) - 1: 0} if other else {},
+        own_kernel,
+        out_shape=outs,
+        in_specs=[SM] + [VM] * 5,
+        out_specs=specs,
+        scratch_shapes=scratch,
+        compiler_params=params(12),
+        name="update_own",
+    )(place, w, left, scale, right, tokens)
+    return new, decs
+
+
+def update_other(place, grid, w, scale, tokens, invs, rights, raws, out, shares):
+    outs, specs, scratch = update_shapes(w, tokens, shares)
+    args = (place, w, scale, tokens, *invs, *rights, *raws, out)
+    rank = scale.shape[1]
+    new, *decs = pl.pallas_call(
+        functools.partial(other_kernel, grid=grid, shares=shares),
+        out_shape=outs,
+        in_specs=[SM] + [VM] * (len(args) - 2) + [HB],
+        out_specs=specs,
+        input_output_aliases={len(args) - 1: 0},
         scratch_shapes=[
             pltpu.VMEM((rank, rank), f32),
-            pltpu.VMEM((rank, half), bf16),
-            pltpu.VMEM((WSLOTS, ch, half), f32),
-            pltpu.VMEM((batch, half), f32),
-            DMA((WSLOTS,)),
+            pltpu.VMEM((rank, w.shape[1]), bf16),
+            pltpu.VMEM((w.shape[0], rank), bf16),
         ]
-        + ([pltpu.VMEM((width, half), f32), DMA((width // ch,))] if other else []),
-        compiler_params=params(18 if other else 9),
-        name="update_other" if other else "update_own",
+        + scratch,
+        compiler_params=params(14),
+        name="update_other",
     )(*args)
     return new, decs
 
@@ -488,14 +680,13 @@
         width, hid = momentum.shape[1], momentum.shape[2]
         swap = peers(ngrp, 1)
         q_h = gather_blocks(factor_q[0].astype(bf16), "row", nrow, row, 1)
-        buffer, parts = load_left(place, momentum[0], gradient[0], q_h, ncol)
-        parts = [parts[k] for k in range(ncol)]
-        got = send_all(parts, "col", ncol)
+        grid = Grid(ncol, width // ncol)
         weights = in_hbm(weights)
-        w_own = fetch(place, weights, parts[0])
-        block = block_sum([parts[0]] + got)
-        raw, gram = join_gram(place, [block] + send_all([block] * ncol, "col", ncol))
-        raw_other = lax.ppermute(raw, "grp", swap)
+        buffer, heads, tails = load_left(place, momentum[0], gradient[0], q_h, grid)
+
+        raw, gram, raws, w_own, w_other = sum_scatter_gather(
+            place, grid, heads, tails, swap, lambda after, s: fetch(place, weights, after, s)
+        )
         gram = sum_over(gram, "row", nrow)
         rr, rr_h = raw_right(raw, buffer)
         for k in bits_of(nrow)[:-1]:
@@ -504,7 +695,7 @@
         rr_other = lax.ppermute(rr_h, "row", peers(nrow, bits_of(nrow)[-1]))
         inv_l, inv_part = chol_inv(place, gram, nrow)
         inv_part = lax.ppermute(inv_part, "grp", swap)
-        left_h, right, right_h, right_own, half_part, squares = factors(
+        left, left_h, right, right_h, right_own, half_part, squares = factors(
             place, raw, inv_l, rr, rr_other, ngrp, nrow
         )
         half_part = lax.ppermute(half_part, "grp", swap)
@@ -520,16 +711,14 @@
         inv_norm_other = lax.ppermute(inv_norm, "grp", swap)
         q_share = factor_share(place, right, inv_norm, factor_q.shape[2])
         scale, mom_new = lax.optimization_barrier((step_size * inv_norm, mom_new))
-        new_weights, dec = update(
-            place, w_own, raw, scale, tokens, [inv_l], [right_own], None, nrow
-        )
+        new_weights, dec = update_own(place, w_own, left, scale, right_own, tokens, nrow)
         inv_part, half_part, mom_new = lax.optimization_barrier(
             (inv_part, half_part, mom_new)
         )
         invs = [inv_part] + send_all([inv_part] * nrow, "row", nrow)
         halves = [half_part] + send_all([half_part] * nrow, "row", nrow)
-        new_weights, dec_other = update(
-            place, weights, raw_other, step_size * inv_norm_other, tokens, invs, halves,
+        new_weights, dec_other = update_other(
+            place, grid, w_other, step_size * inv_norm_other, tokens, invs, halves, raws,
             new_weights, nrow,
         )
         dec[1:] = send_all(dec, "row", nrow)

time: 138 us -> 126 us (0.913)
  starting transfers between devices: 43.4 us -> 36.7 us
  waiting for transfers between devices: 34.7 us -> 30.2 us
    ppermute x18 -> x4, waiting for transfers between devices: 28.6 us -> 0.83 us  [send_all(): return [lax.ppermute(blocks[k], axis, peers(n, k)) for k in range(1, n)]]
    ppermute x18 -> x4, starting transfers between devices: 28.5 us -> 0.84 us  [send_all(): return [lax.ppermute(blocks[k], axis, peers(n, k)) for k in range(1, n)]]
    ppermute x1 -> x19, starting transfers between devices: 1.6 us -> 26.4 us  [the longest x12 17.7 us: send_z(): lax.ppermute(b, 'col', peers(self.n, k * self.nx))]
    ppermute x1 -> x19, waiting for transfers between devices: 0.01 us -> 22.3 us  [the longest x12 15.7 us: send_z(): lax.ppermute(b, 'col', peers(self.n, k * self.nx))]
    ppermute x3, starting transfers between devices: 9.03 us -> 4.74 us  [step(): squares = squares + lax.ppermute(squares, 'col', peers(ncol, k))]
    pallas_call x7 -> x10, Pallas kernels: 32.1 us -> 31.5 us  [the longest x1 9.64 us: load_left(): pl.pallas_call(functools.partial(load_kernel, grid=grid), out_shape=(pltp...]
  transfers between devices with their start and end apart: 28 -> 32, of which waited for: 11 -> 13; matrix products, arithmetic and copies ran while one was open for 0% -> 0% of each run, Pallas kernels for 30% -> 32%
where the time goes in v2:
time: 126 us
  Pallas kernels  55.1 us (44%)
  starting transfers between devices  36.7 us (29%)
  waiting for transfers between devices  30.2 us (24%)
  other arithmetic  2.85 us (2%)
    ppermute x12, starting transfers between devices, send_z(): lax.ppermute(b, 'col', peers(self.n, k * self.nx))  17.7 us
    ppermute x12, waiting for transfers between devices, send_z(): lax.ppermute(b, 'col', peers(self.n, k * self.nx))  15.7 us
    pallas_call x1, Pallas kernels, load_left(): pl.pallas_call(functools.partial(load_kernel, grid=grid), out_shape=(pltp...  9.64 us
    pallas_call x4, Pallas kernels, apply_feedback(): pl.pallas_call(functools.partial(feedback_kernel, lo=lo, hi=hi, ch=ch), o...  9.46 us
    pallas_call x1, Pallas kernels, chol_inv(): pl.pallas_call(chol_inv_kernel, out_shape=(pltpu.VMEM((n, n), f32), pltpu...  8.11 us
    pallas_call x2, Pallas kernels, fetch(): pl.pallas_call(functools.partial(fetch_kernel, other=other), out_shape=pl...  8.03 us
    ppermute x4, waiting for transfers between devices, send_x(): lax.ppermute(b, 'col', peers(self.n, k))  6.64 us
    pallas_call x1, Pallas kernels, update_other(): pl.pallas_call(functools.partial(other_kernel, grid=grid, shares=shares),...  5.67 us
  transfers between devices with their start and end apart: 32, of which 13 were waited for; matrix products, arithmetic and copies ran while one was open for 0% of the time, Pallas kernels for 32%

profile of v2, /device:TPU:0, one launch (start us, length us, event | category | flops | bytes accessed | tf_op | source)
XLA Modules:
  0.0 125.7 jit_solution(491364824039979336)
XLA Ops:
  0.6 1.3 %convert_bitcast_fusion = bf16[2048,128]{1,0:T(8,128)(2,1)S(1)} fusion(f32[1,2048,128]{2,1,0:T(8,128)} %param.7), kind=kLoop, calls=%fused_computation.1 | loop fusion | flops 262144 | bytes 1572864 | tf_op jit(solution)/shard_map/convert_element_type | solution.py:682
  2.5 1.5 %collective-permute-done = bf16[2048,128]{1,0:T(8,128)(2,1)S(1)} collective-permute-done((bf16[2048,128]{1,0:T(8,128)(2,1)S(1)}, bf16[2048,128]{1,0:T(8,128)(2,1)S(1)}, u32[]{:S(2)}, u32[]{:S(2)}) %collective-permute-start) | collective-permute-done | bytes 524320 | tf_op jit(solution)/shard_map/ppermute | solution.py:30
  4.0 1.3 %broadcast_select_fusion.1 = (bf16[2048,128]{1,0:T(8,128)(2,1)S(1)}, bf16[2048,128]{1,0:T(8,128)(2,1)S(1)}) fusion(bf16[2048,128]{1,0:T(8,128)(2,1)S(1)} %collective-permute-done, pred[]{:T(512)S(6)} %ne.3, f32[1,2048,128]{2,1,0:T(8,128)} %param.7), kind=kLoop, calls=%fused_computation.3 | loop fusion | flops 786432 | bytes 2621441 | tf_op jit(solution)/shard_map/jit(_where)/select_n | solution.py:32
  5.5 9.6 %load_left.1 = (f32[2048,2048]{1,0:T(8,128)S(1)}, bf16[704,256]{1,0:T(8,128)(2,1)S(1)}, bf16[704,256]{1,0:T(8,128)(2,1)S(1)}, bf16[160,256]{1,0:T(8,128)(2,1)S(1...) custom-call(s32[3]{0:T(128)S(1)} %pad_add_fusion.at_ref, ...), custom_call_target="tpu_custom_call" | custom-call | tf_op jit(solution)/shard_map/load_left/pallas_call | solution.py:198
  15.1 2.9 %collective-permute-start.1 = (bf16[704,256]{1,0:T(8,128)(2,1)S(1)}, bf16[704,256]{1,0:T(8,128)(2,1)S(1)}, u32[]{:S(2)}, u32[]{:S(2)}) collective-permute-start(bf16[704,256]{1,0:T(8,128)(2,1)S(1)} %get-tuple-element.47), channel_id=1, source_target_pairs={{0,2},{2,0},{4,6},{6,4},{8,10},{10,8},{12,14},{14,12},{1,3},{3,1},... | collective-permute-start | bytes 1081352 | tf_op jit(solution)/shard_map/ppermute | solution.py:55
  18.0 1.6 %collective-permute-start.2 = (bf16[160,256]{1,0:T(8,128)(2,1)S(1)}, bf16[160,256]{1,0:T(8,128)(2,1)S(1)}, u32[]{:S(2)}, u32[]{:S(2)}) collective-permute-start(bf16[160,256]{1,0:T(8,128)(2,1)S(1)} %get-tuple-element.49), channel_id=1, source_target_pairs={{0,4},{2,6},{4,0},{6,2},{8,12},{10,14},{12,8},{14,10},{1,5},{3,7},... | collective-permute-start | bytes 245768 | tf_op jit(solution)/shard_map/ppermute | solution.py:58
  19.6 2.6 %collective-permute-start.3 = (bf16[160,256]{1,0:T(8,128)(2,1)S(1)}, bf16[160,256]{1,0:T(8,128)(2,1)S(1)}, u32[]{:S(2)}, u32[]{:S(2)}) collective-permute-start(bf16[160,256]{1,0:T(8,128)(2,1)S(1)} %get-tuple-element.50), channel_id=1, source_target_pairs={{0,8},{2,10},{4,12},{6,14},{8,0},{10,2},{12,4},{14,6},{1,9},{3,11}... | collective-permute-start | bytes 245768 | tf_op jit(solution)/shard_map/ppermute | solution.py:58
  22.5 6.4 %collective-permute-done.3.refs_4_ = bf16[160,256]{1,0:T(8,128)(2,1)S(1)} collective-permute-done((bf16[160,256]{1,0:T(8,128)(2,1)S(1)}, bf16[160,256]{1,0:T(8,128)(2,1)S(1)}, u32[]{:S(2)}, u32[]{:S(2)}) %collective-permute-start.3) | collective-permute-done | bytes 81952 | tf_op jit(solution)/shard_map/ppermute | solution.py:58
  28.9 1.5 %collective-permute-start.5 = (bf16[176,256]{1,0:T(8,128)(2,1)S(1)}, bf16[176,256]{1,0:T(8,128)(2,1)S(1)}, u32[]{:S(2)}, u32[]{:S(2)}) collective-permute-start(bf16[176,256]{1,0:T(8,128)(2,1)S(1)} %get-tuple-element.53), channel_id=1, source_target_pairs={{0,4},{2,6},{4,0},{6,2},{8,12},{10,14},{12,8},{14,10},{1,5},{3,7},... | collective-permute-start | bytes 270344 | tf_op jit(solution)/shard_map/ppermute | solution.py:58
  30.5 1.6 %collective-permute-start.6 = (bf16[176,256]{1,0:T(8,128)(2,1)S(1)}, bf16[176,256]{1,0:T(8,128)(2,1)S(1)}, u32[]{:S(2)}, u32[]{:S(2)}) collective-permute-start(bf16[176,256]{1,0:T(8,128)(2,1)S(1)} %get-tuple-element.54), channel_id=1, source_target_pairs={{0,8},{2,10},{4,12},{6,14},{8,0},{10,2},{12,4},{14,6},{1,9},{3,11}... | collective-permute-start | bytes 270344 | tf_op jit(solution)/shard_map/ppermute | solution.py:58
  32.0 1.4 %collective-permute-start.7 = (bf16[176,256]{1,0:T(8,128)(2,1)S(1)}, bf16[176,256]{1,0:T(8,128)(2,1)S(1)}, u32[]{:S(2)}, u32[]{:S(2)}) collective-permute-start(bf16[176,256]{1,0:T(8,128)(2,1)S(1)} %get-tuple-element.55), channel_id=1, source_target_pairs={{0,12},{2,14},{4,8},{6,10},{8,4},{10,6},{12,0},{14,2},{1,13},{3,15... | collective-permute-start | bytes 270344 | tf_op jit(solution)/shard_map/ppermute | solution.py:58
  33.9 3.5 %collective-permute-done.8.refs_5_ = bf16[80,256]{1,0:T(8,128)(2,1)S(1)} collective-permute-done((bf16[80,256]{1,0:T(8,128)(2,1)S(1)}, bf16[80,256]{1,0:T(8,128)(2,1)S(1)}, u32[]{:S(2)}, u32[]{:S(2)}) %collective-permute-start.8) | collective-permute-done | bytes 40992 | tf_op jit(solution)/shard_map/ppermute | solution.py:55
  37.4 1.9 %collective-permute-done.6.refs_2_ = bf16[176,256]{1,0:T(8,128)(2,1)S(1)} collective-permute-done((bf16[176,256]{1,0:T(8,128)(2,1)S(1)}, bf16[176,256]{1,0:T(8,128)(2,1)S(1)}, u32[]{:S(2)}, u32[]{:S(2)}) %collective-permute-start.6) | collective-permute-done | bytes 90144 | tf_op jit(solution)/shard_map/ppermute | solution.py:58
  39.4 1.6 %collective-permute-start.9 = (bf16[176,256]{1,0:T(8,128)(2,1)S(1)}, bf16[176,256]{1,0:T(8,128)(2,1)S(1)}, u32[]{:S(2)}, u32[]{:S(2)}) collective-permute-start(bf16[176,256]{1,0:T(8,128)(2,1)S(1)} %get-tuple-element.58.refs_0_.after_ref), channel_id=1, source_target_pairs={{0,4},{2,6},{4,0},{6,2},{8,12},{10,14},{12,8},{14,10},{1,5},{3,7},... | collective-permute-start | bytes 270344 | tf_op jit(solution)/shard_map/ppermute | solution.py:58
  41.0 1.2 collective-permute-start.10
  42.2 1.7 %collective-permute-start.11 = (bf16[176,256]{1,0:T(8,128)(2,1)S(1)}, bf16[176,256]{1,0:T(8,128)(2,1)S(1)}, u32[]{:S(2)}, u32[]{:S(2)}) collective-permute-start(bf16[176,256]{1,0:T(8,128)(2,1)S(1)} %get-tuple-element.58.refs_0_.after_ref), channel_id=1, source_target_pairs={{0,12},{2,14},{4,8},{6,10},{8,4},{10,6},{12,0},{14,2},{1,13},{3,15... | collective-permute-start | bytes 270344 | tf_op jit(solution)/shard_map/ppermute | solution.py:58
  43.8 0.8 collective-permute-start.12
  44.7 3.2 %collective-permute-done.12.refs_5_ = bf16[80,256]{1,0:T(8,128)(2,1)S(1)} collective-permute-done((bf16[80,256]{1,0:T(8,128)(2,1)S(1)}, bf16[80,256]{1,0:T(8,128)(2,1)S(1)}, u32[]{:S(2)}, u32[]{:S(2)}) %collective-permute-start.12) | collective-permute-done | bytes 40992 | tf_op jit(solution)/shard_map/ppermute | solution.py:55
  47.8 1.9 %collective-permute-done.10.refs_2_ = bf16[176,256]{1,0:T(8,128)(2,1)S(1)} collective-permute-done((bf16[176,256]{1,0:T(8,128)(2,1)S(1)}, bf16[176,256]{1,0:T(8,128)(2,1)S(1)}, u32[]{:S(2)}, u32[]{:S(2)}) %collective-permute-start.10) | collective-permute-done | bytes 90144 | tf_op jit(solution)/shard_map/ppermute | solution.py:58
  50.5 1.6 %collective-permute-start.14 = (bf16[160,256]{1,0:T(8,128)(2,1)S(1)}, bf16[160,256]{1,0:T(8,128)(2,1)S(1)}, u32[]{:S(2)}, u32[]{:S(2)}) collective-permute-start(bf16[160,256]{1,0:T(8,128)(2,1)S(1)} %get-tuple-element.61.refs_2_), channel_id=1, source_target_pairs={{0,4},{2,6},{4,0},{6,2},{8,12},{10,14},{12,8},{14,10},{1,5},{3,7},... | collective-permute-start | bytes 245768 | tf_op jit(solution)/shard_map/ppermute | solution.py:58
  52.1 1.1 collective-permute-start.15
  53.3 1.7 %collective-permute-start.16 = (bf16[160,256]{1,0:T(8,128)(2,1)S(1)}, bf16[160,256]{1,0:T(8,128)(2,1)S(1)}, u32[]{:S(2)}, u32[]{:S(2)}) collective-permute-start(bf16[160,256]{1,0:T(8,128)(2,1)S(1)} %get-tuple-element.61.refs_2_), channel_id=1, source_target_pairs={{0,12},{2,14},{4,8},{6,10},{8,4},{10,6},{12,0},{14,2},{1,13},{3,15... | collective-permute-start | bytes 245768 | tf_op jit(solution)/shard_map/ppermute | solution.py:58
  55.6 4.8 %collective-permute-done.15.refs_4_ = bf16[160,256]{1,0:T(8,128)(2,1)S(1)} collective-permute-done((bf16[160,256]{1,0:T(8,128)(2,1)S(1)}, bf16[160,256]{1,0:T(8,128)(2,1)S(1)}, u32[]{:S(2)}, u32[]{:S(2)}) %collective-permute-start.15) | collective-permute-done | bytes 81952 | tf_op jit(solution)/shard_map/ppermute | solution.py:58
  60.4 1.1 join_gram.1
  61.5 2.5 %raw_right.1 = (f32[256,2048]{1,0:T(8,128)S(1)}, bf16[256,2048]{1,0:T(8,128)(2,1)S(1)}) custom-call(bf16[2048,256]{1,0:T(8,128)(2,1)S(1)} %get-tuple-element.64.raw_ref, f32[2048,2048]{1,0:T(8,128)S(1)} %get-tuple-element.66.buf_ref), custom_call_target="tpu_custom_call" | custom-call | tf_op jit(solution)/shard_map/raw_right/pallas_call | solution.py:392
  64.6 1.5 %collective-permute-start.29 = (bf16[1184,256]{1,0:T(8,128)(2,1)S(1)}, bf16[1184,256]{1,0:T(8,128)(2,1)S(1)}, u32[]{:S(2)}, u32[]{:S(2)}) collective-permute-start(bf16[1184,256]{1,0:T(8,128)(2,1)S(1)} %get-tuple-element.78), channel_id=1, source_target_pairs={{0,1},{1,0},{2,3},{3,2},{4,5},{5,4},{6,7},{7,6},{8,9},{9,8},{10,11... | collective-permute-start | bytes 1818632 | tf_op jit(solution)/shard_map/ppermute | solution.py:375
  66.1 1.0 collective-permute-done.17
  67.2 8.1 %chol_inv.1 = (f32[256,256]{1,0:T(8,128)S(1)}, f32[128,256]{1,0:T(8,128)S(1)}) custom-call(s32[3]{0:T(128)S(1)} %pad_add_fusion.at_ref, f32[256,256]{1,0:T(8,128)S(1)} %add.18.g_ref), custom_call_target="tpu_custom_call" | custom-call | tf_op jit(solution)/shard_map/chol_inv/pallas_call | solution.py:117
  75.3 2.4 %factors.1 = (f32[2048,256]{1,0:T(8,128)S(1)}, bf16[2048,256]{1,0:T(8,128)(2,1)S(1)}, f32[256,2048]{1,0:T(8,128)S(1)}, bf16[256,2048]{1,0:T(8,128)(2,1)S(1)}, bf...) custom-call(s32[3]{0:T(128)S(1)} %pad_add_fusion.at_ref, ...), custom_call_target="tpu_custom_call" | custom-call | tf_op jit(solution)/shard_map/factors/pallas_call | solution.py:431
  77.8 1.5 %collective-permute-start.20 = (bf16[128,1024]{1,0:T(8,128)(2,1)S(1)}, bf16[128,1024]{1,0:T(8,128)(2,1)S(1)}, u32[]{:S(2)}, u32[]{:S(2)}) collective-permute-start(bf16[128,1024]{1,0:T(8,128)(2,1)S(1)} %get-tuple-element.69), channel_id=1, source_target_pairs={{0,1},{1,0},{2,3},{3,2},{4,5},{5,4},{6,7},{7,6},{8,9},{9,8},{10,11... | collective-permute-start | bytes 786440 | tf_op jit(solution)/shard_map/ppermute | solution.py:701
  79.3 1.3 %collective-permute-start.21 = (f32[8,256]{1,0:T(8,128)S(1)}, f32[8,256]{1,0:T(8,128)S(1)}, u32[]{:S(2)}, u32[]{:S(2)}) collective-permute-start(f32[8,256]{1,0:T(8,128)S(1)} %get-tuple-element.70), channel_id=1, source_target_pairs={{0,2},{2,0},{4,6},{6,4},{8,10},{10,8},{12,14},{14,12},{1,3},{3,1},... | collective-permute-start | bytes 24584 | tf_op jit(solution)/shard_map/ppermute | solution.py:708
  80.6 2.4 %collective-permute-done.21 = f32[8,256]{1,0:T(8,128)S(1)} collective-permute-done((f32[8,256]{1,0:T(8,128)S(1)}, f32[8,256]{1,0:T(8,128)S(1)}, u32[]{:S(2)}, u32[]{:S(2)}) %collective-permute-start.21) | collective-permute-done | bytes 8224 | tf_op jit(solution)/shard_map/ppermute | solution.py:708
  83.0 1.4 %collective-permute-start.22 = (f32[8,256]{1,0:T(8,128)S(1)}, f32[8,256]{1,0:T(8,128)S(1)}, u32[]{:S(2)}, u32[]{:S(2)}) collective-permute-start(f32[8,256]{1,0:T(8,128)S(1)} %add.19), channel_id=1, source_target_pairs={{0,4},{2,6},{4,0},{6,2},{8,12},{10,14},{12,8},{14,10},{1,5},{3,7},... | collective-permute-start | bytes 24584 | tf_op jit(solution)/shard_map/ppermute | solution.py:708
  84.4 2.2 %collective-permute-done.22 = f32[8,256]{1,0:T(8,128)S(1)} collective-permute-done((f32[8,256]{1,0:T(8,128)S(1)}, f32[8,256]{1,0:T(8,128)S(1)}, u32[]{:S(2)}, u32[]{:S(2)}) %collective-permute-start.22) | collective-permute-done | bytes 8224 | tf_op jit(solution)/shard_map/ppermute | solution.py:708
  86.6 2.0 %collective-permute-start.23 = (f32[8,256]{1,0:T(8,128)S(1)}, f32[8,256]{1,0:T(8,128)S(1)}, u32[]{:S(2)}, u32[]{:S(2)}) collective-permute-start(f32[8,256]{1,0:T(8,128)S(1)} %add.20), channel_id=1, source_target_pairs={{0,8},{2,10},{4,12},{6,14},{8,0},{10,2},{12,4},{14,6},{1,9},{3,11}... | collective-permute-start | bytes 24584 | tf_op jit(solution)/shard_map/ppermute | solution.py:708
  89.2 1.5 %collective-permute-start.18 = (f32[128,256]{1,0:T(8,128)S(1)}, f32[128,256]{1,0:T(8,128)S(1)}, u32[]{:S(2)}, u32[]{:S(2)}) collective-permute-start(f32[128,256]{1,0:T(8,128)S(1)} %get-tuple-element.63), channel_id=1, source_target_pairs={{0,1},{1,0},{2,3},{3,2},{4,5},{5,4},{6,7},{7,6},{8,9},{9,8},{10,11... | collective-permute-start | bytes 393224 | tf_op jit(solution)/shard_map/ppermute | solution.py:697
  90.7 2.4 %feedback.4.rest_0_ = f32[2048,2048]{1,0:T(8,128)} custom-call(f32[2048,2048]{1,0:T(8,128)S(1)} %get-tuple-element.66.buf_ref, bf16[2048,256]{1,0:T(8,128)(2,1)S(1)} %get-tuple-element.71.left_ref, bf16[256,2048]{1,0:T(8,128)(2,1)S(1)} %get-tuple-element.72.right_ref), custom_call_target="tpu_custom_call" | custom-call | tf_op jit(solution)/shard_map/feedback/pallas_call | solution.py:493
  93.1 2.4 %feedback.5.rest_0_ = f32[2048,2048]{1,0:T(8,128)} custom-call(f32[2048,2048]{1,0:T(8,128)S(1)} %get-tuple-element.66.buf_ref, bf16[2048,256]{1,0:T(8,128)(2,1)S(1)} %get-tuple-element.71.left_ref, bf16[256,2048]{1,0:T(8,128)(2,1)S(1)} %get-tuple-element.72.right_ref, f32[2048,2048]{1,0:T(8,128)} %feedback.4.rest_0_), custom_call_target="tpu_custom_call", output_to_operand_aliasing={{}: (3, {})} | custom-call | tf_op jit(solution)/shard_map/feedback/pallas_call | solution.py:493
  95.4 2.4 %feedback.6.rest_0_ = f32[2048,2048]{1,0:T(8,128)} custom-call(f32[2048,2048]{1,0:T(8,128)S(1)} %get-tuple-element.66.buf_ref, bf16[2048,256]{1,0:T(8,128)(2,1)S(1)} %get-tuple-element.71.left_ref, bf16[256,2048]{1,0:T(8,128)(2,1)S(1)} %get-tuple-element.72.right_ref, f32[2048,2048]{1,0:T(8,128)} %feedback.5.rest_0_), custom_call_target="tpu_custom_call", output_to_operand_aliasing={{}: (3, {})} | custom-call | tf_op jit(solution)/shard_map/feedback/pallas_call | solution.py:493
  97.8 2.4 %feedback.7 = f32[2048,2048]{1,0:T(8,128)} custom-call(f32[2048,2048]{1,0:T(8,128)S(1)} %get-tuple-element.66.buf_ref, bf16[2048,256]{1,0:T(8,128)(2,1)S(1)} %get-tuple-element.71.left_ref, bf16[256,2048]{1,0:T(8,128)(2,1)S(1)} %get-tuple-element.72.right_ref, f32[2048,2048]{1,0:T(8,128)} %feedback.6.rest_0_), custom_call_target="tpu_custom_call", output_to_operand_aliasing={{}: (3, {})} | custom-call | tf_op jit(solution)/shard_map/feedback/pallas_call | solution.py:493
  100.9 4.0 %fetch_weights.3.w_ref = f32[2048,1024]{1,0:T(8,128)S(1)} custom-call(s32[3]{0:T(128)S(1)} %pad_add_fusion.at_ref, f32[2,2048,1024]{2,1,0:T(8,128)} %w_ref.3, bf16[704,256]{1,0:T(8,128)(2,1)S(1)} %get-tuple-element.46.refs_0_.after_ref), custom_call_target="tpu_custom_call" | custom-call | tf_op jit(solution)/shard_map/fetch_weights/pallas_call | solution.py:235
  104.9 4.0 %fetch_weights.2.w_ref = f32[2048,1024]{1,0:T(8,128)S(1)} custom-call(s32[3]{0:T(128)S(1)} %pad_add_fusion.at_ref, f32[2,2048,1024]{2,1,0:T(8,128)} %w_ref.3, bf16[176,256]{1,0:T(8,128)(2,1)S(1)} %get-tuple-element.58.refs_0_.after_ref), custom_call_target="tpu_custom_call" | custom-call | tf_op jit(solution)/shard_map/fetch_weights/pallas_call | solution.py:235
  108.9 1.6 %collective-permute-start.28 = (bf16[160,256]{1,0:T(8,128)(2,1)S(1)}, bf16[160,256]{1,0:T(8,128)(2,1)S(1)}, u32[]{:S(2)}, u32[]{:S(2)}) collective-permute-start(bf16[160,256]{1,0:T(8,128)(2,1)S(1)} %get-tuple-element.61.refs_2_), channel_id=1, source_target_pairs={{0,1},{1,0},{2,3},{3,2},{4,5},{5,4},{6,7},{7,6},{8,9},{9,8},{10,11... | collective-permute-start | bytes 245768 | tf_op jit(solution)/shard_map/ppermute | solution.py:369
  110.5 4.4 %update_own.1 = (f32[2,2048,1024]{2,1,0:T(8,128)}, f32[128,1024]{1,0:T(8,128)S(1)}, f32[128,1024]{1,0:T(8,128)S(1)}) custom-call(s32[3]{0:T(128)S(1)} %pad_add_fusion.at_ref, f32[2048,1024]{1,0:T(8,128)S(1)} %fetch_weights.3.w_ref, f32[2048,256]{1,0:T(8,128)S(1)} %get-tuple-element.79.left_ref, f32[8,256]{1,0:T(8,128)S(1)} %get-tuple-element.80.scale_ref, ...), custom_call_target="tpu_custom_call" | custom-call | tf_op jit(solution)/shard_map/update_own/pallas_call | solution.py:617
  115.5 0.8 collective-permute-done.25.rest_1_
  116.3 5.7 %update_other.1 = (f32[2,2048,1024]{2,1,0:T(8,128)}, f32[128,1024]{1,0:T(8,128)S(1)}, f32[128,1024]{1,0:T(8,128)S(1)}) custom-call(s32[3]{0:T(128)S(1)} %pad_add_fusion.at_ref, f32[2048,1024]{1,0:T(8,128)S(1)} %fetch_weights.2.w_ref, f32[8,256]{1,0:T(8,128)S(1)} %broadcast_multiply_fusion.scale_ref, ...), custom_call_target="tpu_custom_call", output_to_operand_aliasing={{0}: (11, {})} | custom-call | tf_op jit(solution)/shard_map/update_other/pallas_call | solution.py:633
  122.2 2.0 %factor_share.1 = f32[2048,128]{1,0:T(8,128)} custom-call(s32[3]{0:T(128)S(1)} %pad_add_fusion.at_ref, f32[256,2048]{1,0:T(8,128)S(1)} %get-tuple-element.75.right_ref, f32[8,256]{1,0:T(8,128)S(1)} %get-tuple-element.89.norm_ref), custom_call_target="tpu_custom_call" | custom-call | tf_op jit(solution)/shard_map/factor_share/pallas_call | solution.py:459
  124.3 1.5 %finish.1 = bf16[128,1024]{1,0:T(8,128)(2,1)} custom-call(s32[3]{0:T(128)S(1)} %pad_add_fusion.at_ref, f32[128,1024]{1,0:T(8,128)S(1)} %get-tuple-element.84.refs_0_, f32[128,1024]{1,0:T(8,128)S(1)} %collective-permute-done.30.refs_1_, f32[128,1024]{1,0:T(8,128)S(1)} %get-tuple-element.86.refs_2_, f32[128,1024]{1,0:T(8,128)S(1)} %collective-permute-done.31.refs_3_), custom_call_target="tpu_custom_call" | custom-call | tf_op jit(solution)/shard_map/finish/pallas_call | solution.py:663
  (45 shorter events, 5.8 us)
Async XLA Ops:
  1.9 2.1 %collective-permute-start = (bf16[2048,128]{1,0:T(8,128)(2,1)S(1)}, bf16[2048,128]{1,0:T(8,128)(2,1)S(1)}, u32[]{:S(2)}, u32[]{:S(2)}) collective-permute-start(bf16[2048,128]{1,0:T(8,128)(2,1)S(1)} %convert_bitcast_fusion), channel_id=1, source_target_pairs={{0,16},{16,0},{1,17},{17,1},{2,18},{18,2},{3,19},{19,3},{4,20},{20... | collective-permute-start | bytes 1572872 | tf_op jit(solution)/shard_map/ppermute | solution.py:30
  15.1 13.7 %collective-permute-start.1 = (bf16[704,256]{1,0:T(8,128)(2,1)S(1)}, bf16[704,256]{1,0:T(8,128)(2,1)S(1)}, u32[]{:S(2)}, u32[]{:S(2)}) collective-permute-start(bf16[704,256]{1,0:T(8,128)(2,1)S(1)} %get-tuple-element.47), channel_id=1, source_target_pairs={{0,2},{2,0},{4,6},{6,4},{8,10},{10,8},{12,14},{14,12},{1,3},{3,1},... | collective-permute-start | bytes 1081352 | tf_op jit(solution)/shard_map/ppermute | solution.py:55
  18.0 4.4 %collective-permute-start.2 = (bf16[160,256]{1,0:T(8,128)(2,1)S(1)}, bf16[160,256]{1,0:T(8,128)(2,1)S(1)}, u32[]{:S(2)}, u32[]{:S(2)}) collective-permute-start(bf16[160,256]{1,0:T(8,128)(2,1)S(1)} %get-tuple-element.49), channel_id=1, source_target_pairs={{0,4},{2,6},{4,0},{6,2},{8,12},{10,14},{12,8},{14,10},{1,5},{3,7},... | collective-permute-start | bytes 245768 | tf_op jit(solution)/shard_map/ppermute | solution.py:58
  19.6 9.2 %collective-permute-start.3 = (bf16[160,256]{1,0:T(8,128)(2,1)S(1)}, bf16[160,256]{1,0:T(8,128)(2,1)S(1)}, u32[]{:S(2)}, u32[]{:S(2)}) collective-permute-start(bf16[160,256]{1,0:T(8,128)(2,1)S(1)} %get-tuple-element.50), channel_id=1, source_target_pairs={{0,8},{2,10},{4,12},{6,14},{8,0},{10,2},{12,4},{14,6},{1,9},{3,11}... | collective-permute-start | bytes 245768 | tf_op jit(solution)/shard_map/ppermute | solution.py:58
  22.2 6.6 %collective-permute-start.4 = (bf16[160,256]{1,0:T(8,128)(2,1)S(1)}, bf16[160,256]{1,0:T(8,128)(2,1)S(1)}, u32[]{:S(2)}, u32[]{:S(2)}) collective-permute-start(bf16[160,256]{1,0:T(8,128)(2,1)S(1)} %get-tuple-element.51), channel_id=1, source_target_pairs={{0,12},{2,14},{4,8},{6,10},{8,4},{10,6},{12,0},{14,2},{1,13},{3,15... | collective-permute-start | bytes 245768 | tf_op jit(solution)/shard_map/ppermute | solution.py:58
  28.9 8.5 %collective-permute-start.5 = (bf16[176,256]{1,0:T(8,128)(2,1)S(1)}, bf16[176,256]{1,0:T(8,128)(2,1)S(1)}, u32[]{:S(2)}, u32[]{:S(2)}) collective-permute-start(bf16[176,256]{1,0:T(8,128)(2,1)S(1)} %get-tuple-element.53), channel_id=1, source_target_pairs={{0,4},{2,6},{4,0},{6,2},{8,12},{10,14},{12,8},{14,10},{1,5},{3,7},... | collective-permute-start | bytes 270344 | tf_op jit(solution)/shard_map/ppermute | solution.py:58
  30.5 8.9 %collective-permute-start.6 = (bf16[176,256]{1,0:T(8,128)(2,1)S(1)}, bf16[176,256]{1,0:T(8,128)(2,1)S(1)}, u32[]{:S(2)}, u32[]{:S(2)}) collective-permute-start(bf16[176,256]{1,0:T(8,128)(2,1)S(1)} %get-tuple-element.54), channel_id=1, source_target_pairs={{0,8},{2,10},{4,12},{6,14},{8,0},{10,2},{12,4},{14,6},{1,9},{3,11}... | collective-permute-start | bytes 270344 | tf_op jit(solution)/shard_map/ppermute | solution.py:58
  32.0 7.3 %collective-permute-start.7 = (bf16[176,256]{1,0:T(8,128)(2,1)S(1)}, bf16[176,256]{1,0:T(8,128)(2,1)S(1)}, u32[]{:S(2)}, u32[]{:S(2)}) collective-permute-start(bf16[176,256]{1,0:T(8,128)(2,1)S(1)} %get-tuple-element.55), channel_id=1, source_target_pairs={{0,12},{2,14},{4,8},{6,10},{8,4},{10,6},{12,0},{14,2},{1,13},{3,15... | collective-permute-start | bytes 270344 | tf_op jit(solution)/shard_map/ppermute | solution.py:58
  33.4 4.0 %collective-permute-start.8 = (bf16[80,256]{1,0:T(8,128)(2,1)S(1)}, bf16[80,256]{1,0:T(8,128)(2,1)S(1)}, u32[]{:S(2)}, u32[]{:S(2)}) collective-permute-start(bf16[80,256]{1,0:T(8,128)(2,1)S(1)} %get-tuple-element.57), channel_id=1, source_target_pairs={{0,2},{2,0},{4,6},{6,4},{8,10},{10,8},{12,14},{14,12},{1,3},{3,1},... | collective-permute-start | bytes 122888 | tf_op jit(solution)/shard_map/ppermute | solution.py:55
  39.4 8.5 %collective-permute-start.9 = (bf16[176,256]{1,0:T(8,128)(2,1)S(1)}, bf16[176,256]{1,0:T(8,128)(2,1)S(1)}, u32[]{:S(2)}, u32[]{:S(2)}) collective-permute-start(bf16[176,256]{1,0:T(8,128)(2,1)S(1)} %get-tuple-element.58.refs_0_.after_ref), channel_id=1, source_target_pairs={{0,4},{2,6},{4,0},{6,2},{8,12},{10,14},{12,8},{14,10},{1,5},{3,7},... | collective-permute-start | bytes 270344 | tf_op jit(solution)/shard_map/ppermute | solution.py:58
  41.0 8.8 %collective-permute-start.10 = (bf16[176,256]{1,0:T(8,128)(2,1)S(1)}, bf16[176,256]{1,0:T(8,128)(2,1)S(1)}, u32[]{:S(2)}, u32[]{:S(2)}) collective-permute-start(bf16[176,256]{1,0:T(8,128)(2,1)S(1)} %get-tuple-element.58.refs_0_.after_ref), channel_id=1, source_target_pairs={{0,8},{2,10},{4,12},{6,14},{8,0},{10,2},{12,4},{14,6},{1,9},{3,11}... | collective-permute-start | bytes 270344 | tf_op jit(solution)/shard_map/ppermute | solution.py:58
  42.2 7.6 %collective-permute-start.11 = (bf16[176,256]{1,0:T(8,128)(2,1)S(1)}, bf16[176,256]{1,0:T(8,128)(2,1)S(1)}, u32[]{:S(2)}, u32[]{:S(2)}) collective-permute-start(bf16[176,256]{1,0:T(8,128)(2,1)S(1)} %get-tuple-element.58.refs_0_.after_ref), channel_id=1, source_target_pairs={{0,12},{2,14},{4,8},{6,10},{8,4},{10,6},{12,0},{14,2},{1,13},{3,15... | collective-permute-start | bytes 270344 | tf_op jit(solution)/shard_map/ppermute | solution.py:58
  43.8 4.0 %collective-permute-start.12 = (bf16[80,256]{1,0:T(8,128)(2,1)S(1)}, bf16[80,256]{1,0:T(8,128)(2,1)S(1)}, u32[]{:S(2)}, u32[]{:S(2)}) collective-permute-start(bf16[80,256]{1,0:T(8,128)(2,1)S(1)} %get-tuple-element.59.refs_4_), channel_id=1, source_target_pairs={{0,2},{2,0},{4,6},{6,4},{8,10},{10,8},{12,14},{14,12},{1,3},{3,1},... | collective-permute-start | bytes 122888 | tf_op jit(solution)/shard_map/ppermute | solution.py:55
  49.8 10.6 %collective-permute-start.13 = (bf16[704,256]{1,0:T(8,128)(2,1)S(1)}, bf16[704,256]{1,0:T(8,128)(2,1)S(1)}, u32[]{:S(2)}, u32[]{:S(2)}) collective-permute-start(bf16[704,256]{1,0:T(8,128)(2,1)S(1)} %get-tuple-element.60.refs_0_), channel_id=1, source_target_pairs={{0,2},{2,0},{4,6},{6,4},{8,10},{10,8},{12,14},{14,12},{1,3},{3,1},... | collective-permute-start | bytes 1081352 | tf_op jit(solution)/shard_map/ppermute | solution.py:55
  50.5 5.0 %collective-permute-start.14 = (bf16[160,256]{1,0:T(8,128)(2,1)S(1)}, bf16[160,256]{1,0:T(8,128)(2,1)S(1)}, u32[]{:S(2)}, u32[]{:S(2)}) collective-permute-start(bf16[160,256]{1,0:T(8,128)(2,1)S(1)} %get-tuple-element.61.refs_2_), channel_id=1, source_target_pairs={{0,4},{2,6},{4,0},{6,2},{8,12},{10,14},{12,8},{14,10},{1,5},{3,7},... | collective-permute-start | bytes 245768 | tf_op jit(solution)/shard_map/ppermute | solution.py:58
  52.1 8.3 %collective-permute-start.15 = (bf16[160,256]{1,0:T(8,128)(2,1)S(1)}, bf16[160,256]{1,0:T(8,128)(2,1)S(1)}, u32[]{:S(2)}, u32[]{:S(2)}) collective-permute-start(bf16[160,256]{1,0:T(8,128)(2,1)S(1)} %get-tuple-element.61.refs_2_), channel_id=1, source_target_pairs={{0,8},{2,10},{4,12},{6,14},{8,0},{10,2},{12,4},{14,6},{1,9},{3,11}... | collective-permute-start | bytes 245768 | tf_op jit(solution)/shard_map/ppermute | solution.py:58
  53.3 7.2 %collective-permute-start.16 = (bf16[160,256]{1,0:T(8,128)(2,1)S(1)}, bf16[160,256]{1,0:T(8,128)(2,1)S(1)}, u32[]{:S(2)}, u32[]{:S(2)}) collective-permute-start(bf16[160,256]{1,0:T(8,128)(2,1)S(1)} %get-tuple-element.61.refs_2_), channel_id=1, source_target_pairs={{0,12},{2,14},{4,8},{6,10},{8,4},{10,6},{12,0},{14,2},{1,13},{3,15... | collective-permute-start | bytes 245768 | tf_op jit(solution)/shard_map/ppermute | solution.py:58
  64.1 11.3 %collective-permute-start.19 = (bf16[256,2048]{1,0:T(8,128)(2,1)S(1)}, bf16[256,2048]{1,0:T(8,128)(2,1)S(1)}, u32[]{:S(2)}, u32[]{:S(2)}) collective-permute-start(bf16[256,2048]{1,0:T(8,128)(2,1)S(1)} %get-tuple-element.68), channel_id=1, source_target_pairs={{0,16},{16,0},{1,17},{17,1},{2,18},{18,2},{3,19},{19,3},{4,20},{20... | collective-permute-start | bytes 3145736 | tf_op jit(solution)/shard_map/ppermute | solution.py:695
  64.1 3.0 %collective-permute-start.17 = (f32[256,256]{1,0:T(8,128)S(1)}, f32[256,256]{1,0:T(8,128)S(1)}, u32[]{:S(2)}, u32[]{:S(2)}) collective-permute-start(f32[256,256]{1,0:T(8,128)S(1)} %get-tuple-element.62), channel_id=1, source_target_pairs={{0,16},{16,0},{1,17},{17,1},{2,18},{18,2},{3,19},{19,3},{4,20},{20... | collective-permute-start | bytes 786440 | tf_op jit(solution)/shard_map/ppermute | solution.py:38
  64.6 50.9 %collective-permute-start.29 = (bf16[1184,256]{1,0:T(8,128)(2,1)S(1)}, bf16[1184,256]{1,0:T(8,128)(2,1)S(1)}, u32[]{:S(2)}, u32[]{:S(2)}) collective-permute-start(bf16[1184,256]{1,0:T(8,128)(2,1)S(1)} %get-tuple-element.78), channel_id=1, source_target_pairs={{0,1},{1,0},{2,3},{3,2},{4,5},{5,4},{6,7},{7,6},{8,9},{9,8},{10,11... | collective-permute-start | bytes 1818632 | tf_op jit(solution)/shard_map/ppermute | solution.py:375
  77.8 22.5 %collective-permute-start.20 = (bf16[128,1024]{1,0:T(8,128)(2,1)S(1)}, bf16[128,1024]{1,0:T(8,128)(2,1)S(1)}, u32[]{:S(2)}, u32[]{:S(2)}) collective-permute-start(bf16[128,1024]{1,0:T(8,128)(2,1)S(1)} %get-tuple-element.69), channel_id=1, source_target_pairs={{0,1},{1,0},{2,3},{3,2},{4,5},{5,4},{6,7},{7,6},{8,9},{9,8},{10,11... | collective-permute-start | bytes 786440 | tf_op jit(solution)/shard_map/ppermute | solution.py:701
  79.3 3.7 %collective-permute-start.21 = (f32[8,256]{1,0:T(8,128)S(1)}, f32[8,256]{1,0:T(8,128)S(1)}, u32[]{:S(2)}, u32[]{:S(2)}) collective-permute-start(f32[8,256]{1,0:T(8,128)S(1)} %get-tuple-element.70), channel_id=1, source_target_pairs={{0,2},{2,0},{4,6},{6,4},{8,10},{10,8},{12,14},{14,12},{1,3},{3,1},... | collective-permute-start | bytes 24584 | tf_op jit(solution)/shard_map/ppermute | solution.py:708
  83.0 3.7 %collective-permute-start.22 = (f32[8,256]{1,0:T(8,128)S(1)}, f32[8,256]{1,0:T(8,128)S(1)}, u32[]{:S(2)}, u32[]{:S(2)}) collective-permute-start(f32[8,256]{1,0:T(8,128)S(1)} %add.19), channel_id=1, source_target_pairs={{0,4},{2,6},{4,0},{6,2},{8,12},{10,14},{12,8},{14,10},{1,5},{3,7},... | collective-permute-start | bytes 24584 | tf_op jit(solution)/shard_map/ppermute | solution.py:708
  86.6 13.6 %collective-permute-start.23 = (f32[8,256]{1,0:T(8,128)S(1)}, f32[8,256]{1,0:T(8,128)S(1)}, u32[]{:S(2)}, u32[]{:S(2)}) collective-permute-start(f32[8,256]{1,0:T(8,128)S(1)} %add.20), channel_id=1, source_target_pairs={{0,8},{2,10},{4,12},{6,14},{8,0},{10,2},{12,4},{14,6},{1,9},{3,11}... | collective-permute-start | bytes 24584 | tf_op jit(solution)/shard_map/ppermute | solution.py:708
  88.7 26.9 %collective-permute-start.27 = (bf16[704,256]{1,0:T(8,128)(2,1)S(1)}, bf16[704,256]{1,0:T(8,128)(2,1)S(1)}, u32[]{:S(2)}, u32[]{:S(2)}) collective-permute-start(bf16[704,256]{1,0:T(8,128)(2,1)S(1)} %get-tuple-element.60.refs_0_), channel_id=1, source_target_pairs={{0,1},{1,0},{2,3},{3,2},{4,5},{5,4},{6,7},{7,6},{8,9},{9,8},{10,11... | collective-permute-start | bytes 1081352 | tf_op jit(solution)/shard_map/ppermute | solution.py:369
  89.2 11.0 %collective-permute-start.18 = (f32[128,256]{1,0:T(8,128)S(1)}, f32[128,256]{1,0:T(8,128)S(1)}, u32[]{:S(2)}, u32[]{:S(2)}) collective-permute-start(f32[128,256]{1,0:T(8,128)S(1)} %get-tuple-element.63), channel_id=1, source_target_pairs={{0,1},{1,0},{2,3},{3,2},{4,5},{5,4},{6,7},{7,6},{8,9},{9,8},{10,11... | collective-permute-start | bytes 393224 | tf_op jit(solution)/shard_map/ppermute | solution.py:697
  100.2 16.1 %collective-permute-start.26 = (bf16[128,1024]{1,0:T(8,128)(2,1)S(1)}, bf16[128,1024]{1,0:T(8,128)(2,1)S(1)}, u32[]{:S(2)}, u32[]{:S(2)}) collective-permute-start(bf16[128,1024]{1,0:T(8,128)(2,1)S(1)} %collective-permute-done.20.rest_2_), channel_id=1, source_target_pairs={{0,16},{16,0},{1,17},{17,1},{2,18},{18,2},{3,19},{19,3},{4,20},{20... | collective-permute-start | bytes 786440 | tf_op jit(solution)/shard_map/ppermute | solution.py:43
  100.3 14.6 %collective-permute-start.24 = (f32[8,256]{1,0:T(8,128)S(1)}, f32[8,256]{1,0:T(8,128)S(1)}, u32[]{:S(2)}, u32[]{:S(2)}) collective-permute-start(f32[8,256]{1,0:T(8,128)S(1)} %get-tuple-element.89.norm_ref), channel_id=1, source_target_pairs={{0,1},{1,0},{2,3},{3,2},{4,5},{5,4},{6,7},{7,6},{8,9},{9,8},{10,11... | collective-permute-start | bytes 24584 | tf_op jit(solution)/shard_map/ppermute | solution.py:711
  104.9 5.6 %copy-start = (bf16[256,2048]{1,0:T(8,128)(2,1)S(1)}, bf16[256,2048]{1,0:T(8,128)(2,1)}, u32[]{:S(2)}) copy-start(bf16[256,2048]{1,0:T(8,128)(2,1)} %tok_ref.3) | copy-start | bytes 3145732
  108.9 6.1 %collective-permute-start.28 = (bf16[160,256]{1,0:T(8,128)(2,1)S(1)}, bf16[160,256]{1,0:T(8,128)(2,1)S(1)}, u32[]{:S(2)}, u32[]{:S(2)}) collective-permute-start(bf16[160,256]{1,0:T(8,128)(2,1)S(1)} %get-tuple-element.61.refs_2_), channel_id=1, source_target_pairs={{0,1},{1,0},{2,3},{3,2},{4,5},{5,4},{6,7},{7,6},{8,9},{9,8},{10,11... | collective-permute-start | bytes 245768 | tf_op jit(solution)/shard_map/ppermute | solution.py:369
  114.9 1.4 %collective-permute-start.25 = (f32[128,256]{1,0:T(8,128)S(1)}, f32[128,256]{1,0:T(8,128)S(1)}, u32[]{:S(2)}, u32[]{:S(2)}) collective-permute-start(f32[128,256]{1,0:T(8,128)S(1)} %collective-permute-done.18.rest_0_), channel_id=1, source_target_pairs={{0,16},{16,0},{1,17},{17,1},{2,18},{18,2},{3,19},{19,3},{4,20},{20... | collective-permute-start | bytes 393224 | tf_op jit(solution)/shard_map/ppermute | solution.py:43
  115.0 9.3 %collective-permute-start.30 = (f32[128,1024]{1,0:T(8,128)S(1)}, f32[128,1024]{1,0:T(8,128)S(1)}, u32[]{:S(2)}, u32[]{:S(2)}) collective-permute-start(f32[128,1024]{1,0:T(8,128)S(1)} %get-tuple-element.85), channel_id=1, source_target_pairs={{0,16},{16,0},{1,17},{17,1},{2,18},{18,2},{3,19},{19,3},{4,20},{20... | collective-permute-start | bytes 1572872 | tf_op jit(solution)/shard_map/ppermute | solution.py:43
  122.0 2.3 %collective-permute-start.31 = (f32[128,1024]{1,0:T(8,128)S(1)}, f32[128,1024]{1,0:T(8,128)S(1)}, u32[]{:S(2)}, u32[]{:S(2)}) collective-permute-start(f32[128,1024]{1,0:T(8,128)S(1)} %get-tuple-element.87), channel_id=1, source_target_pairs={{0,16},{16,0},{1,17},{17,1},{2,18},{18,2},{3,19},{19,3},{4,20},{20... | collective-permute-start | bytes 1572872 | tf_op jit(solution)/shard_map/ppermute | solution.py:43
